TPU v7x, 32 devices: a whole 2x2x4 slice. The times are simulated.
32 devices in a mesh: blk: 16 (over z, x, core), grp: 2 (over y).
Axes of the slice: x: 2, y: 2, z: 4, core: 2. Of those that a mesh axis runs over, the one named last changes fastest.
Arguments:
- orbitals: float32 [32, 110592], P(('blk', 'grp')), may hold values from -6 to 6
- occupation: float32 [32], P(('blk', 'grp')), may hold values from 0.2 to 2
Outputs:
- exchange: float32 [32, 110592], P(('blk', 'grp'))
- energy: float32 [], replicated
All inputs are finite; a program needn't handle non-finite values.
Results may differ from a plain program's by a relative error of at most 0.00012.
Values sent between devices are 32-bit elements; how exact they have to be, the bound alone decides.
No kernel may reach another device: no remote copies, remote signals or barrier semaphores. Data moves between devices by JAX's collectives and lax.ppermute only.
A program may use at most 64 MiB of HBM per device.

v0:
```python
import math

import jax
import jax.numpy as jnp
from jax import lax
from jax.sharding import PartitionSpec as P

GRID = 48


mixing = 0.25
screening = 0.1


def from_behind(value, axis, steps):
    count = lax.axis_size(axis)
    pairs = [(source, (source + steps) % count) for source in range(count)]
    return lax.ppermute(value, axis, pairs)


def tables(extent):
    indices = jnp.arange(extent, dtype=jnp.int32)
    product = indices[:, None] * indices[None, :] % extent
    angles = product.astype(jnp.float32) * (2.0 * math.pi / extent)
    cosine = jnp.cos(angles)
    sine = jnp.sin(angles)
    first = jnp.stack([cosine, -sine], axis=1)
    forward = jnp.stack(
        [jnp.stack([cosine, -sine], axis=1), jnp.stack([sine, cosine], axis=1)], axis=0
    )
    inverse = jnp.stack(
        [jnp.stack([cosine, sine], axis=1), jnp.stack([-sine, cosine], axis=1)], axis=0
    )
    last = jnp.stack([cosine, -sine], axis=0)
    return (first, forward, inverse, last)


def kernel_table(extent):
    indices = jnp.arange(extent, dtype=jnp.int32)
    folded = (indices + extent // 2) % extent - extent // 2
    squared = (folded.astype(jnp.float32) * (2.0 * math.pi / extent)) ** 2
    return 1.0 / (
        squared[:, None, None] + squared[None, :, None] + squared[None, None, :] + screening
    )


def along_first(values, table):
    return jnp.einsum("pcxyz,cxdk->pdkyz", values, table, precision=lax.Precision.HIGHEST)


def along_second(values, table):
    return jnp.einsum("pcxyz,cydk->pdxkz", values, table, precision=lax.Precision.HIGHEST)


def pair_potential(single, partners, transforms, kernel):
    first, forward, inverse, last = transforms
    density = (single[None, :] * partners).reshape(-1, GRID, GRID, GRID)
    stacked = jnp.einsum("pxyz,zck->pcxyk", density, first, precision=lax.Precision.HIGHEST)
    stacked = along_second(stacked, forward)
    stacked = along_first(stacked, forward)
    stacked = stacked * kernel[None, None]
    stacked = along_first(stacked, inverse)
    stacked = along_second(stacked, inverse)
    potential = jnp.einsum(
        "pcxyz,czk->pxyk", stacked, last, precision=lax.Precision.HIGHEST
    ) / float(GRID**3)
    return potential.reshape(partners.shape)


def local(orbitals, occupation):
    transforms = tables(GRID)
    kernel = kernel_table(GRID)
    visiting = from_behind((orbitals, occupation), "blk", 1)
    partners, weights = (
        lax.all_gather(visiting[0], "grp", axis=0, tiled=True),
        lax.all_gather(visiting[1], "grp", axis=0, tiled=True),
    )

    def scan_step(carried, item):
        single, single_weight = item
        potential = pair_potential(single, partners, transforms, kernel)
        own_part = jnp.sum(weights[:, None] * partners * potential, axis=0)
        return (carried + single_weight * single[None, :] * potential, own_part)

    start = jnp.zeros(partners.shape, jnp.float32)
    carried, collected = lax.scan(scan_step, start, (orbitals, occupation))
    returned = lax.psum_scatter(carried, "grp", scatter_dimension=0, tiled=True)
    collected = collected + from_behind(returned, "blk", -1)
    exchange = -mixing * collected
    total_orbitals = orbitals.shape[0] * lax.axis_size(("blk", "grp"))
    local_energy = jnp.sum(occupation[:, None] * orbitals * exchange)
    energy = lax.psum(local_energy, ("blk", "grp")) / (2.0 * float(GRID**3) * total_orbitals)
    return (exchange, energy)


def solution(mesh):
    placed = (P(("blk", "grp"), None), P(("blk", "grp")))
    return jax.shard_map(
        local, mesh=mesh, in_specs=placed, out_specs=(P(("blk", "grp"), None), P()), check_vma=False
    )
```

profile of v0, /device:TPU:0, one launch (start us, length us, event | category | flops | bytes accessed | tf_op | source)
XLA Modules:
  0.0 196.6 jit_solution(12694306188467929370)
XLA Ops:
  7.2 0.0 copy-start.1
  7.2 0.0 all-reduce.4.cloned.1.call-start
  7.2 0.5 collective-permute-start.1
  7.8 2.6 %collective-permute-start = (f32[1]{0:T(128)}, f32[1]{0:T(128)}, u32[]{:S(2)}, u32[]{:S(2)}) collective-permute-start(f32[1]{0:T(128)} %param.3), channel_id=1, source_target_pairs={{0,2},{2,4},{4,6},{6,8},{8,10},{10,12},{12,14},{14,16},{16,18},{18... | collective-permute-start | bytes 20 | tf_op jit(solution)/shard_map/ppermute | solution.py:18
  10.4 0.7 fusion.35
  11.1 0.7 fusion.34
  11.8 0.7 fusion.36
  12.6 0.1 sine_negate_fusion
  13.4 2.1 %broadcast_multiply_fusion.1 = f32[1,110592]{1,0:T(1,128)} fusion(f32[1,110592]{1,0:T(1,128)} %param.2, f32[]{:T(128)} %bitcast.79), kind=kLoop, calls=%fused_computation.23 | loop fusion | flops 110592 | bytes 884740 | tf_op jit(solution)/shard_map/while/body/eval_jaxpr/mul | solution.py:83
  15.5 0.2 fusion.19
  15.6 1.4 fusion.42
  17.0 0.1 maximum_bitcast_fusion
  17.1 0.1 broadcast_add_fusion
  17.2 1.4 add_divide_fusion
  18.5 0.5 collective-permute-done
  19.0 1.3 dynamic-update-slice
  20.3 0.1 copy.6
  20.4 4.9 %all-reduce = f32[2]{0:T(128)S(1)} all-reduce(f32[2]{0:T(128)S(1)} %dynamic-update-slice), channel_id=1, replica_groups=mesh['blk'=16,'grp'=2] {'grp'}, use_global_device_ids=true, to_apply=%add | all-reduce | flops 2 | bytes 16
  25.4 0.0 collective-permute-done.1
  25.4 11.5 %all-gather = f32[2,1,110592]{2,1,0:T(1,128)S(1)} all-gather(f32[1,1,110592]{2,1,0:T(1,128)S(1)} %bitcast.84), channel_id=1, replica_groups=mesh['blk'=16,'grp'=2] {'grp'}, dimensions={0}, use_global_device_ids=true | all-gather | bytes 1327104 | tf_op jit(solution)/shard_map/all_gather | solution.py:75
  36.8 0.0 copy-done.1
  36.8 1.8 bitcast_multiply_fusion.2
  38.7 2.4 %reshape.219 = f32[2,48,48,48,1]{3,2,1,0,4:T(8,128)S(1)} reshape(f32[2,110592]{1,0:T(2,128)} %bitcast_multiply_fusion.2) | data formatting | bytes 1769472 | tf_op jit(solution)/shard_map/while/body/eval_jaxpr/reshape | solution.py:57
  41.1 8.6 %fusion.22 = f32[2,48,2,48,48]{4,1,3,2,0:T(8,128)S(1)} fusion(f32[2,48,48,48,1]{3,2,1,0,4:T(8,128)S(1)} %reshape.219, f32[48,2,48,1,1]{2,1,0,3,4:T(2,128)S(1)} %get-tuple-element.48), kind=kOutput, calls=%fused_computation.39 | convolution fusion | flops 254803968 | bytes 2672640 | tf_op jit(solution)/shard_map/while/body/eval_jaxpr/pxyz,zck->pcxyk/dot_general | solution.py:58
  49.7 10.7 %fusion.9 = f32[2,48,2,48,48,1]{3,1,5,4,2,0:T(8,128)} fusion(f32[2,48,2,48,1,1]{1,3,0,5,4,2:T(8,128)S(1)} %copy.6, f32[2,48,2,48,48]{4,1,3,2,0:T(8,128)S(1)} %fusion.22), kind=kOutput, calls=%fused_computation.11 | convolution fusion | flops 509607936 | bytes 3575808 | tf_op jit(solution)/shard_map/while/body/eval_jaxpr/pcxyz,cydk->pdxkz/dot_general | solution.py:52
  60.4 6.5 %copy.8 = f32[2,48,2,48,48,1]{4,3,2,1,0,5:T(8,128)} copy(f32[2,48,2,48,48,1]{3,1,5,4,2,0:T(8,128)} %fusion.9) | data formatting | bytes 3538944 | tf_op jit(solution)/shard_map/while/body/eval_jaxpr/pcxyz,cydk->pdxkz/dot_general | solution.py:52
  66.9 0.0 copy-start
  66.9 6.4 %fusion.7 = f32[2,48,2,48,48,1]{4,1,5,3,2,0:T(8,128)S(1)} fusion(f32[2,48,2,48,1,1]{1,3,0,5,4,2:T(8,128)S(1)} %copy.6, f32[2,48,2,48,48,1]{4,3,2,1,0,5:T(8,128)} %copy.8), kind=kOutput, calls=%fused_computation.9 | convolution fusion | flops 509607936 | bytes 3575808 | tf_op jit(solution)/shard_map/while/body/eval_jaxpr/pcxyz,cxdk->pdkyz/dot_general | solution.py:48
  73.3 0.0 copy-done
  73.3 1.5 fusion.2
  74.8 6.9 %fusion.5 = f32[2,48,2,48,48,1]{4,1,5,3,2,0:T(8,128)S(1)} fusion(f32[2,2,48,48,48,1]{4,3,0,2,1,5:T(8,128)S(1)} %fusion.2, f32[2,48,2,48,1,1]{3,2,1,0,4,5:T(2,128)S(1)} %get-tuple-element.52), kind=kOutput, calls=%fused_computation.7 | convolution fusion | flops 509607936 | bytes 3575808 | tf_op jit(solution)/shard_map/while/body/eval_jaxpr/pcxyz,cxdk->pdkyz/dot_general | solution.py:48
  81.7 5.9 %fusion.3 = f32[2,48,2,48,48,1]{4,1,5,0,3,2:T(8,128)S(1)} fusion(f32[2,48,2,48,1,1]{3,2,1,0,4,5:T(2,128)S(1)} %get-tuple-element.52, f32[2,48,2,48,48,1]{4,1,5,3,2,0:T(8,128)S(1)} %fusion.5), kind=kOutput, calls=%fused_computation.4 | convolution fusion | flops 509607936 | bytes 3575808 | tf_op jit(solution)/shard_map/while/body/eval_jaxpr/pcxyz,cydk->pdxkz/dot_general | solution.py:52
  87.6 3.8 %bitcast_multiply_fusion.1 = f32[2,48,48,48]{3,2,1,0:T(8,128)S(1)} fusion(f32[2,48,2,48,48,1]{4,1,5,0,3,2:T(8,128)S(1)} %fusion.3, f32[1,48,48]{2,1,0:T(8,128)S(1)} %get-tuple-element.54, f32[1,48,48]{2,1,0:T(8,128)S(1)} %get-tuple-element.55), kind=kOutput, calls=%fused_computation.14 | convolution fusion | flops 255029760 | bytes 2672640 | tf_op jit(solution)/shard_map/while/body/eval_jaxpr/pcxyz,czk->pxyk/dot_general | solution.py:64
  91.4 2.9 %reshape.210 = f32[2,110592]{1,0:T(2,128)} reshape(f32[2,48,48,48]{3,2,1,0:T(8,128)S(1)} %bitcast_multiply_fusion.1) | data formatting | bytes 1769472 | tf_op jit(solution)/shard_map/while/body/eval_jaxpr/reshape | solution.py:67
  94.3 0.0 copy-start.2
  94.3 3.6 %broadcast_multiply_fusion = (f32[2,110592]{1,0:T(2,128)}, f32[110592]{0:T(1024)S(1)}) fusion(f32[2,110592]{1,0:T(2,128)} %reshape.210, f32[110592]{0:T(1024)} %bitcast.82, f32[2,1,110592]{2,1,0:T(1,128)S(1)} %all-gather, f32[2]{0:T(128)S(1)} %all-reduce), kind=kLoop, calls=%fused_computation.22 | loop fusion | flops 774144 | bytes 3538952 | tf_op jit(solution)/shard_map/while/body/eval_jaxpr/mul | solution.py:83
  97.9 0.0 all-reduce.4.cloned.1.call-update
  97.9 37.0 %all-reduce.4.cloned.1.call-done = f32[2,110592]{1,0:T(2,128)} async-done(((f32[2,110592]{1,0:T(2,128)}), f32[2,110592]{1,0:T(2,128)}) %all-reduce.4.cloned.1.call-update) | async-done | bytes 884752
  134.9 2.2 %constant_dynamic-slice_fusion = f32[1,110592]{1,0:T(1,128)S(1)} fusion(f32[2,110592]{1,0:T(2,128)} %all-reduce.4.cloned.1.call-done, u32[]{:T(128)} %bitcast.39), kind=kLoop, calls=%fused_computation.63 | loop fusion | bytes 884740
  137.1 3.6 %collective-permute-start.2 = (f32[1,110592]{1,0:T(1,128)S(1)}, f32[1,110592]{1,0:T(1,128)S(1)}, u32[]{:S(2)}, u32[]{:S(2)}) collective-permute-start(f32[1,110592]{1,0:T(1,128)S(1)} %constant_dynamic-slice_fusion), channel_id=1, source_target_pairs={{0,30},{2,0},{4,2},{6,4},{8,6},{10,8},{12,10},{14,12},{16,14},{18,... | collective-permute-start | bytes 1327112 | tf_op jit(solution)/shard_map/ppermute | solution.py:18
  140.7 5.8 %collective-permute-done.2 = f32[1,110592]{1,0:T(1,128)S(1)} collective-permute-done((f32[1,110592]{1,0:T(1,128)S(1)}, f32[1,110592]{1,0:T(1,128)S(1)}, u32[]{:S(2)}, u32[]{:S(2)}) %collective-permute-start.2) | collective-permute-done | bytes 442400 | tf_op jit(solution)/shard_map/ppermute | solution.py:18
  146.5 0.0 copy-done.2
  146.5 2.3 %multiply_reduce_fusion = (f32[]{:T(128)}, f32[1,110592]{1,0:T(1,128)}) fusion(f32[1,110592]{1,0:T(1,128)S(1)} %bitcast.83, f32[1,110592]{1,0:T(1,128)S(1)} %collective-permute-done.2, f32[1,110592]{1,0:T(1,128)S(1)} %copy-done.2, f32[]{:T(128)} %bitcast.80), kind=kLoop, calls=%fused_computation.20 | loop fusion | flops 552959 | bytes 1769480 | tf_op jit(solution)/shard_map/reduce_sum | solution.py:91
  148.8 38.9 %psum.7 = f32[]{:T(128)} all-reduce(f32[]{:T(128)} %get-tuple-element.26), channel_id=1, replica_groups=mesh['blk'=16,'grp'=2] {'blk','grp'}, use_global_device_ids=true, to_apply=%region_3.4 | all-reduce | flops 1 | bytes 8 | tf_op jit(solution)/shard_map/psum | solution.py:92
  (2 shorter events, 0.0 us)
Async XLA Ops:
  7.2 29.7 %copy-start.1 = (f32[1,110592]{1,0:T(1,128)S(1)}, f32[1,110592]{1,0:T(1,128)}, u32[]{:S(2)}) copy-start(f32[1,110592]{1,0:T(1,128)} %param.2) | copy-start | bytes 1327108
  7.2 127.8 %all-reduce.4.cloned.1.call-start = ((), (), s32[]{:S(2)}) async-start(), calls=%async_computation | async-start | bytes 1769472
  7.2 18.2 %collective-permute-start.1 = (f32[1,110592]{1,0:T(1,128)}, f32[1,110592]{1,0:T(1,128)S(1)}, u32[]{:S(2)}, u32[]{:S(2)}) collective-permute-start(f32[1,110592]{1,0:T(1,128)} %param.2), channel_id=1, source_target_pairs={{0,2},{2,4},{4,6},{6,8},{8,10},{10,12},{12,14},{14,16},{16,18},{18... | collective-permute-start | bytes 1327112 | tf_op jit(solution)/shard_map/ppermute | solution.py:18
  7.8 11.3 %collective-permute-start = (f32[1]{0:T(128)}, f32[1]{0:T(128)}, u32[]{:S(2)}, u32[]{:S(2)}) collective-permute-start(f32[1]{0:T(128)} %param.3), channel_id=1, source_target_pairs={{0,2},{2,4},{4,6},{6,8},{8,10},{10,12},{12,14},{14,16},{16,18},{18... | collective-permute-start | bytes 20 | tf_op jit(solution)/shard_map/ppermute | solution.py:18
  66.9 6.4 %copy-start = (f32[48,48,48]{2,1,0:T(8,128)S(1)}, f32[48,48,48]{2,1,0:T(8,128)}, u32[]{:S(2)}) copy-start(f32[48,48,48]{2,1,0:T(8,128)} %add_divide_fusion) | copy-start | bytes 1327108
  94.3 52.1 %copy-start.2 = (f32[1,110592]{1,0:T(1,128)S(1)}, f32[1,110592]{1,0:T(1,128)}, u32[]{:S(2)}) copy-start(f32[1,110592]{1,0:T(1,128)} %param.2) | copy-start | bytes 1327108
  137.1 9.4 %collective-permute-start.2 = (f32[1,110592]{1,0:T(1,128)S(1)}, f32[1,110592]{1,0:T(1,128)S(1)}, u32[]{:S(2)}, u32[]{:S(2)}) collective-permute-start(f32[1,110592]{1,0:T(1,128)S(1)} %constant_dynamic-slice_fusion), channel_id=1, source_target_pairs={{0,30},{2,0},{4,2},{6,4},{8,6},{10,8},{12,10},{14,12},{16,14},{18,... | collective-permute-start | bytes 1327112 | tf_op jit(solution)/shard_map/ppermute | solution.py:18
Sparse Core Ops, SparseCore 0:
  98.0 36.8 all-reduce.3
where the time goes:
time: 200 us; the launch traced here: 197 us
  blocking collectives  55.3 us (28%)
  waiting for transfers between devices  43.3 us (22%)
  matrix products  42.3 us (21%)
  local copies, waits for them, and re-layouts  16.8 us (8%)
  between operations  16.8 us (8%)
  other arithmetic  15.3 us (8%)
  starting transfers between devices  6.73 us (3%)
    psum x1, blocking collectives, local(): lax.psum(local_energy, ('blk', 'grp'))  38.9 us
    unnamed x2, waiting for transfers between devices  37 us
    dot_general x2, matrix products, along_second(): jnp.einsum('pcxyz,cydk->pdxkz', values, table, precision=lax.Precision.HI...  16.6 us
    dot_general x2, matrix products, along_first(): jnp.einsum('pcxyz,cxdk->pdkyz', values, table, precision=lax.Precision.HI...  13.3 us
    all_gather x1, blocking collectives, local(): lax.all_gather(visiting[0], 'grp', axis=0, tiled=True)  11.5 us
    dot_general x1, matrix products, pair_potential(): jnp.einsum('pxyz,zck->pcxyk', density, first, precision=lax.Precision.HIG...  8.62 us
    ppermute x3, starting transfers between devices, from_behind(): return lax.ppermute(value, axis, pairs)  6.7 us
    dot_general x1, local copies, waits for them, and re-layouts, along_second(): jnp.einsum('pcxyz,cydk->pdxkz', values, table, precision=lax.Precision.HI...  6.51 us
  transfers between devices with their start and end apart: 4, of which 3 were waited for; matrix products, arithmetic and copies ran while one was open for 5% of the time, Pallas kernels for 0%

commit v1 on v0

v1 whole, which is shorter than its diff:
```python
import math
import numpy as np
import jax
import jax.numpy as jnp
from jax import lax
from jax.sharding import PartitionSpec as P
from jax.experimental import pallas as pl
from jax.experimental.pallas import tpu as pltpu

mixing = 0.25
screening = 0.1
LANES = 128
F32 = jnp.float32


def split(values):
    values = np.asarray(values, np.float64)
    high = values.astype(jnp.bfloat16).astype(np.float64)
    low = (values - high).astype(jnp.bfloat16).astype(np.float64)
    return high.astype(np.float32), low.astype(np.float32)


def basis(extent):
    n = np.arange(extent)
    rows, freqs = [], []
    half = extent // 2
    rows += [np.full(extent, math.sqrt(1.0 / extent)), np.where(n % 2 == 0, 1.0, -1.0) * math.sqrt(1.0 / extent)]
    freqs += [0, half]
    for k in range(1, half):
        angle = 2.0 * math.pi * ((k * n) % extent) / extent
        rows += [math.sqrt(2.0 / extent) * np.cos(angle), math.sqrt(2.0 / extent) * np.sin(angle)]
        freqs += [k, k]
    return np.stack(rows), np.array(freqs)


def lane_table(matrix):
    extent = matrix.shape[0]
    high, low = split(matrix)
    table = np.zeros((2 * LANES, 2 * LANES), np.float32)
    for part in range(2):
        for pair in range(2):
            r = part * LANES + pair * extent
            c = pair * extent
            table[r:r + extent, c:c + extent] = high
            table[r:r + extent, LANES + c:LANES + c + extent] = low
    return table


def row_table(matrix):
    high, low = split(matrix)
    return np.concatenate([high, high, low], axis=1)


def low_of(x):
    return x - x.astype(jnp.bfloat16).astype(F32)


def rows_apply(table, x):
    return jnp.dot(table, jnp.concatenate([x, low_of(x), x], axis=0), preferred_element_type=F32)


def lanes_apply(x, table):
    both = jnp.dot(jnp.concatenate([x, low_of(x)], axis=1), table, preferred_element_type=F32)
    return both[:, :LANES] + both[:, LANES:]


def kernel_body(extent, w_own_ref, w_par_ref, w_prev_ref, own_ref, par_ref, prev_ref, fz_ref, iz_ref, fr_ref, ir_ref, kern_ref,
                mine_ref, topar_ref, toprev_ref, e_ref, t_ref):
    pitch = t_ref.shape[0] // extent
    tiles = 3
    per = tiles * LANES // extent
    runs = extent // per
    row_stride = tiles * runs
    lane = lax.broadcasted_iota(jnp.int32, (extent, LANES), 1)
    fr, ir = fr_ref[...], ir_ref[...]

    def dense(ref, y1, t):
        return ref[pl.ds(tiles * y1 + t, extent, stride=row_stride), :]

    def pick(parts, start):
        t, off = divmod(start, LANES)
        if off + extent <= LANES:
            return parts[t], off
        return jnp.where(lane >= off, parts[t], parts[t + 1]), off

    def turn(x, shift):
        shift %= LANES
        return x if shift == 0 else pltpu.roll(x, shift, 1)

    for y1 in range(runs):
        prev = [dense(prev_ref, y1, t) for t in range(tiles)]
        first = [dense(own_ref, y1, t) * prev[t] for t in range(tiles)]
        second = [dense(par_ref, y1, t) * prev[t] for t in range(tiles)]
        rows = []
        for y0 in range(per):
            a, off = pick(first, y0 * extent)
            b, _ = pick(second, y0 * extent)
            rows.append(jnp.where(lane < extent, turn(a, -off), turn(b, extent - off)))
        after = lanes_apply(jnp.concatenate(rows, axis=0), fz_ref[...])
        for y0 in range(0, per, 2):
            two = jnp.concatenate([after[y0 * extent:(y0 + 1) * extent], after[(y0 + 1) * extent:(y0 + 2) * extent]], axis=1)
            out = rows_apply(fr, two)
            y = y1 * per + y0
            t_ref[pl.ds(y * pitch, extent), :] = out[:, :LANES]
            t_ref[pl.ds((y + 1) * pitch, extent), :] = out[:, LANES:]

    for p in range(extent // 2):
        two = jnp.concatenate([t_ref[pl.ds(2 * p, extent, stride=pitch), :], t_ref[pl.ds(2 * p + 1, extent, stride=pitch), :]], axis=1)
        out = rows_apply(fr, two)
        if p == 0:
            k = jnp.concatenate([kern_ref[0], kern_ref[extent // 2]], axis=1)
        else:
            k = jnp.concatenate([kern_ref[p], kern_ref[p]], axis=1)
        out = rows_apply(ir, out * k)
        t_ref[pl.ds(2 * p, extent, stride=pitch), :] = out[:, :LANES]
        t_ref[pl.ds(2 * p + 1, extent, stride=pitch), :] = out[:, LANES:]

    w_own, w_par, w_prev = w_own_ref[0], w_par_ref[0], w_prev_ref[0]
    total = jnp.zeros((extent, LANES), F32)
    for y1 in range(runs):
        rows = []
        for y0 in range(0, per, 2):
            y = y1 * per + y0
            two = jnp.concatenate([t_ref[pl.ds(y * pitch, extent), :], t_ref[pl.ds((y + 1) * pitch, extent), :]], axis=1)
            out = rows_apply(ir, two)
            rows += [out[:, :LANES], out[:, LANES:]]
        after = lanes_apply(jnp.concatenate(rows, axis=0), iz_ref[...])
        pieces = [after[y0 * extent:(y0 + 1) * extent] for y0 in range(per)]
        for t in range(tiles):
            v = [None, None]
            for y0 in range(per):
                start = y0 * extent - t * LANES
                if start >= LANES or start + extent <= 0:
                    continue
                for pair in range(2):
                    moved = turn(pieces[y0], start - pair * extent)
                    v[pair] = moved if v[pair] is None else jnp.where(lane >= start, moved, v[pair])
            prev, own, par = dense(prev_ref, y1, t), dense(own_ref, y1, t), dense(par_ref, y1, t)
            rows_at = pl.ds(tiles * y1 + t, extent, stride=row_stride)
            one, two = w_prev * (prev * v[0]), w_prev * (prev * v[1])
            mine_ref[rows_at, :] = one
            topar_ref[rows_at, :] = two
            toprev_ref[rows_at, :] = (w_own * own) * v[0] + (w_par * par) * v[1]
            total = total + ((w_own * own) * one + (w_par * par) * two)
    e_ref[...] = jnp.full(e_ref.shape, jnp.sum(total), F32)


def pair_call(weights, own, par, prev, count):
    cells = own.size
    extent = round(cells ** (1.0 / 3.0))
    matrix, freqs = basis(extent)
    ksq = (2.0 * math.pi / extent * freqs) ** 2
    kzl = np.zeros(LANES)
    kzl[:extent] = ksq
    kzl[extent:2 * extent] = ksq
    distinct = (2.0 * math.pi / extent * np.arange(extent // 2 + 1)) ** 2
    kern = (1.0 / (distinct[:, None, None] + ksq[None, :, None] + kzl[None, None, :] + screening)).astype(np.float32)
    pitch = extent + 8
    dense = jax.ShapeDtypeStruct((cells // LANES, LANES), F32)
    shape = lambda a: a.reshape(cells // LANES, LANES)
    vm = pl.BlockSpec(memory_space=pltpu.VMEM)
    return pl.pallas_call(
        lambda *refs: kernel_body(extent, *refs),
        out_shape=(dense, dense, dense, jax.ShapeDtypeStruct((count, LANES), F32)),
        in_specs=[pl.BlockSpec(memory_space=pltpu.SMEM)] * 3 + [vm] * 8,
        out_specs=(vm, vm, vm, vm),
        scratch_shapes=[pltpu.VMEM((extent * pitch, LANES), F32)],
        name="pairs",
    )(*weights, shape(own), shape(par), shape(prev), jnp.asarray(lane_table(matrix.T)), jnp.asarray(lane_table(matrix)),
      jnp.asarray(row_table(matrix)), jnp.asarray(row_table(matrix.T)), jnp.asarray(kern))


AXES = ("blk", "grp")


def moved(value, blocks, groups):
    n_blk, n_grp = lax.axis_size("blk"), lax.axis_size("grp")
    pairs = [(b * n_grp + g, (b + blocks) % n_blk * n_grp + (g + groups) % n_grp)
             for b in range(n_blk) for g in range(n_grp)]
    return lax.ppermute(value, AXES, pairs)


def local(orbitals, occupation):
    count = lax.axis_size(AXES)
    cells = orbitals.shape[1]
    partner, w_partner = moved(orbitals, 0, 1), moved(occupation, 0, 1)
    previous, w_previous = moved(orbitals, 1, 0), moved(occupation, 1, 0)
    mine, to_partner, to_previous, shares = pair_call(
        (occupation, w_partner, w_previous), orbitals, partner, previous, count)
    back = moved(to_partner, 0, 1)
    behind = moved(to_previous, -1, 0)
    everyone = lax.all_to_all(shares, AXES, 0, 0, tiled=True)
    exchange = (-mixing * (mine + back + behind)).reshape(1, cells)
    energy = jnp.sum(everyone[:, 0]) * (-2.0 * mixing / (2.0 * cells * orbitals.shape[0] * count))
    return exchange, energy


def solution(mesh):
    return jax.shard_map(local, mesh=mesh, in_specs=(P(AXES, None), P(AXES)),
                         out_specs=(P(AXES, None), P()), check_vma=False)
```

time: 200 us -> 41.8 us (0.21); the launches traced: 197 us -> 41.6 us
  blocking collectives: 55.3 us -> 9.76 us
  matrix products: 42.3 us -> 0 us
  waiting for transfers between devices: 43.3 us -> 8.2 us
  local copies, waits for them, and re-layouts: 16.8 us -> 0.89 us
  between operations: 16.8 us -> 3.1 us
  other arithmetic: 15.3 us -> 2.44 us
  Pallas kernels: 0 us -> 7.12 us
  starting transfers between devices: 6.73 us -> 10 us
    dot_general x6 -> x0, matrix products: 42.3 us -> none  [the longest x2 16.6 us: along_second(): jnp.einsum('pcxyz,cydk->pdxkz', values, table, precision=lax.Precision.HI...]
    psum x1 -> x0, blocking collectives: 38.9 us -> none  [local(): lax.psum(local_energy, ('blk', 'grp'))]
    unnamed x2 -> x0, waiting for transfers between devices: 37 us -> none
    all_gather x1 -> x0, blocking collectives: 11.5 us -> none  [local(): lax.all_gather(visiting[0], 'grp', axis=0, tiled=True)]
    all_to_all x0 -> x1, blocking collectives: none -> 9.76 us  [local(): everyone = lax.all_to_all(shares, AXES, 0, 0, tiled=True)]
    pallas_call x0 -> x1, Pallas kernels: none -> 7.12 us  [pair_call(): pl.pallas_call(lambda *refs: kernel_body(extent, *refs), out_shape=(dense...]
    mul x4 -> x1, other arithmetic: 8.96 us -> 1.84 us  [local(): exchange = (-mixing * (mine + back + behind)).reshape(1, cells)]
    dot_general x1 -> x0, local copies, waits for them, and re-layouts: 6.51 us -> none  [along_second(): jnp.einsum('pcxyz,cydk->pdxkz', values, table, precision=lax.Precision.HI...]
  transfers between devices with their start and end apart: 4 -> 6, of which waited for: 3 -> 1; matrix products, arithmetic and copies ran while one was open for 5% -> 1% of each run, Pallas kernels for 0% -> 0%
where the time goes in v1:
time: 41.8 us; the launch traced here: 41.6 us
  starting transfers between devices  10 us (24%)
  blocking collectives  9.76 us (23%)
  waiting for transfers between devices  8.2 us (20%)
  Pallas kernels  7.12 us (17%)
  between operations  3.1 us (7%)
  other arithmetic  2.44 us (6%)
  local copies, waits for them, and re-layouts  0.89 us (2%)
    ppermute x6, starting transfers between devices, moved(): return lax.ppermute(value, AXES, pairs)  10 us
    all_to_all x1, blocking collectives, local(): everyone = lax.all_to_all(shares, AXES, 0, 0, tiled=True)  9.76 us
    ppermute x6, waiting for transfers between devices, moved(): return lax.ppermute(value, AXES, pairs)  8.2 us
    pallas_call x1, Pallas kernels, pair_call(): pl.pallas_call(lambda *refs: kernel_body(extent, *refs), out_shape=(dense...  7.12 us
    mul x1, other arithmetic, local(): exchange = (-mixing * (mine + back + behind)).reshape(1, cells)  1.84 us
    unnamed x4, local copies, waits for them, and re-layouts  0.89 us
  transfers between devices with their start and end apart: 6, of which 1 were waited for; matrix products, arithmetic and copies ran while one was open for 1% of the time, Pallas kernels for 0%

profile of v1, /device:TPU:0, one launch (start us, length us, event | category | flops | bytes accessed | tf_op | source)
XLA Modules:
  0.0 41.6 jit_solution(18150761494812184489)
XLA Ops:
  0.6 0.5 %collective-permute-start.3 = (f32[1,110592]{1,0:T(1,128)}, f32[1,110592]{1,0:T(1,128)S(1)}, u32[]{:S(2)}, u32[]{:S(2)}) collective-permute-start(f32[1,110592]{1,0:T(1,128)} %param.7), channel_id=1, source_target_pairs={{0,2},{1,3},{2,4},{3,5},{4,6},{5,7},{6,8},{7,9},{8,10},{9,11},{10,... | collective-permute-start | bytes 1327112 | tf_op jit(solution)/shard_map/ppermute | solution.py:180
  1.2 2.6 %collective-permute-start.2 = (f32[1,110592]{1,0:T(1,128)}, f32[1,110592]{1,0:T(1,128)S(1)}, u32[]{:S(2)}, u32[]{:S(2)}) collective-permute-start(f32[1,110592]{1,0:T(1,128)} %param.7), channel_id=1, source_target_pairs={{0,1},{1,0},{2,3},{3,2},{4,5},{5,4},{6,7},{7,6},{8,9},{9,8},{10,11... | collective-permute-start | bytes 1327112 | tf_op jit(solution)/shard_map/ppermute | solution.py:180
  3.8 0.1 collective-permute-start
  3.8 1.4 %collective-permute-start.1 = (f32[1]{0:T(128)}, f32[1]{0:T(128)}, u32[]{:S(2)}, u32[]{:S(2)}) collective-permute-start(f32[1]{0:T(128)} %param.8), channel_id=1, source_target_pairs={{0,2},{1,3},{2,4},{3,5},{4,6},{5,7},{6,8},{7,9},{8,10},{9,11},{10,... | collective-permute-start | bytes 20 | tf_op jit(solution)/shard_map/ppermute | solution.py:180
  5.9 8.2 %collective-permute-done.refs_1_ = f32[1]{0:T(128)} collective-permute-done((f32[1]{0:T(128)}, f32[1]{0:T(128)}, u32[]{:S(2)}, u32[]{:S(2)}) %collective-permute-start) | collective-permute-done | bytes 36 | tf_op jit(solution)/shard_map/ppermute | solution.py:180
  14.1 0.0 collective-permute-done.1.refs_2_
  14.1 0.0 collective-permute-done.3
  14.1 0.0 copy-start
  14.1 0.0 collective-permute-done.2
  14.1 0.0 copy-start.1
  14.1 0.7 %copy-done = f32[1,110592]{1,0:T(1,128)} copy-done((f32[1,110592]{1,0:T(1,128)}, f32[1,110592]{1,0:T(1,128)S(1)}, u32[]{:S(2)}) %copy-start) | copy-done | bytes 442392
  14.8 0.1 copy-done.1
  15.0 7.1 %pairs.1 = (f32[864,128]{1,0:T(8,128)}, f32[864,128]{1,0:T(8,128)}, f32[864,128]{1,0:T(8,128)}, f32[32,128]{1,0:T(8,128)}) custom-call(f32[1]{0:T(128)S(6)} %copy.10.refs_0_, f32[1]{0:T(128)} %collective-permute-done.refs_1_, f32[1]{0:T(128)} %collective-permute-done.1.refs_2_, f32[864,128]{1,0:T(8,128)} %bitcast.9, f32[864,128]{1,0:T(8,128)} %bitcast.11, ...), custom_call_target="tpu_custom_call" | custom-call | tf_op jit(solution)/shard_map/pairs/pallas_call | solution.py:162
  22.1 2.4 %collective-permute-start.4 = (f32[864,128]{1,0:T(8,128)}, f32[864,128]{1,0:T(8,128)S(1)}, u32[]{:S(2)}, u32[]{:S(2)}) collective-permute-start(f32[864,128]{1,0:T(8,128)} %get-tuple-element.7), channel_id=1, source_target_pairs={{0,1},{1,0},{2,3},{3,2},{4,5},{5,4},{6,7},{7,6},{8,9},{9,8},{10,11... | collective-permute-start | bytes 1327112 | tf_op jit(solution)/shard_map/ppermute | solution.py:180
  24.5 3.0 %collective-permute-start.5 = (f32[864,128]{1,0:T(8,128)}, f32[864,128]{1,0:T(8,128)S(1)}, u32[]{:S(2)}, u32[]{:S(2)}) collective-permute-start(f32[864,128]{1,0:T(8,128)} %get-tuple-element.8), channel_id=1, source_target_pairs={{0,30},{1,31},{2,0},{3,1},{4,2},{5,3},{6,4},{7,5},{8,6},{9,7},{10,... | collective-permute-start | bytes 1327112 | tf_op jit(solution)/shard_map/ppermute | solution.py:180
  27.6 9.8 %all_to_all.12 = f32[32,1,128]{2,1,0:T(1,128)S(1)} all-to-all(f32[32,1,128]{2,1,0:T(1,128)} %bitcast.13), channel_id=1, replica_groups=mesh['blk'=16,'grp'=2] {'blk','grp'}, dimensions={0} | all-to-all | bytes 32768 | tf_op jit(solution)/shard_map/all_to_all | solution.py:192
  37.3 0.6 %slice_reduce_fusion = f32[]{:T(128)} fusion(f32[32,128]{1,0:T(8,128)S(1)} %bitcast.12), kind=kLoop, calls=%fused_computation.1 | loop fusion | flops 31 | bytes 132 | tf_op jit(solution)/shard_map/reduce_sum | solution.py:194
  38.6 0.0 collective-permute-done.4
  38.6 0.0 collective-permute-done.5
  38.6 1.8 %add_multiply_fusion = f32[864,128]{1,0:T(8,128)} fusion(f32[864,128]{1,0:T(8,128)S(1)} %collective-permute-done.5, f32[864,128]{1,0:T(8,128)} %get-tuple-element.6, f32[864,128]{1,0:T(8,128)S(1)} %collective-permute-done.4), kind=kLoop, calls=%fused_computation | loop fusion | flops 331776 | bytes 1769472 | tf_op jit(solution)/shard_map/mul | solution.py:193
Async XLA Ops:
  0.6 13.5 %collective-permute-start.3 = (f32[1,110592]{1,0:T(1,128)}, f32[1,110592]{1,0:T(1,128)S(1)}, u32[]{:S(2)}, u32[]{:S(2)}) collective-permute-start(f32[1,110592]{1,0:T(1,128)} %param.7), channel_id=1, source_target_pairs={{0,2},{1,3},{2,4},{3,5},{4,6},{5,7},{6,8},{7,9},{8,10},{9,11},{10,... | collective-permute-start | bytes 1327112 | tf_op jit(solution)/shard_map/ppermute | solution.py:180
  1.2 12.9 %collective-permute-start.2 = (f32[1,110592]{1,0:T(1,128)}, f32[1,110592]{1,0:T(1,128)S(1)}, u32[]{:S(2)}, u32[]{:S(2)}) collective-permute-start(f32[1,110592]{1,0:T(1,128)} %param.7), channel_id=1, source_target_pairs={{0,1},{1,0},{2,3},{3,2},{4,5},{5,4},{6,7},{7,6},{8,9},{9,8},{10,11... | collective-permute-start | bytes 1327112 | tf_op jit(solution)/shard_map/ppermute | solution.py:180
  3.8 10.3 %collective-permute-start = (f32[1]{0:T(128)}, f32[1]{0:T(128)}, u32[]{:S(2)}, u32[]{:S(2)}) collective-permute-start(f32[1]{0:T(128)} %param.8), channel_id=1, source_target_pairs={{0,1},{1,0},{2,3},{3,2},{4,5},{5,4},{6,7},{7,6},{8,9},{9,8},{10,11... | collective-permute-start | bytes 20 | tf_op jit(solution)/shard_map/ppermute | solution.py:180
  3.8 10.2 %collective-permute-start.1 = (f32[1]{0:T(128)}, f32[1]{0:T(128)}, u32[]{:S(2)}, u32[]{:S(2)}) collective-permute-start(f32[1]{0:T(128)} %param.8), channel_id=1, source_target_pairs={{0,2},{1,3},{2,4},{3,5},{4,6},{5,7},{6,8},{7,9},{8,10},{9,11},{10,... | collective-permute-start | bytes 20 | tf_op jit(solution)/shard_map/ppermute | solution.py:180
  14.1 0.8 %copy-start = (f32[1,110592]{1,0:T(1,128)}, f32[1,110592]{1,0:T(1,128)S(1)}, u32[]{:S(2)}) copy-start(f32[1,110592]{1,0:T(1,128)S(1)} %collective-permute-done.3) | copy-start | bytes 1327108
  14.1 0.9 %copy-start.1 = (f32[1,110592]{1,0:T(1,128)}, f32[1,110592]{1,0:T(1,128)S(1)}, u32[]{:S(2)}) copy-start(f32[1,110592]{1,0:T(1,128)S(1)} %collective-permute-done.2) | copy-start | bytes 1327108
  22.1 16.5 %collective-permute-start.4 = (f32[864,128]{1,0:T(8,128)}, f32[864,128]{1,0:T(8,128)S(1)}, u32[]{:S(2)}, u32[]{:S(2)}) collective-permute-start(f32[864,128]{1,0:T(8,128)} %get-tuple-element.7), channel_id=1, source_target_pairs={{0,1},{1,0},{2,3},{3,2},{4,5},{5,4},{6,7},{7,6},{8,9},{9,8},{10,11... | collective-permute-start | bytes 1327112 | tf_op jit(solution)/shard_map/ppermute | solution.py:180
  24.5 14.0 %collective-permute-start.5 = (f32[864,128]{1,0:T(8,128)}, f32[864,128]{1,0:T(8,128)S(1)}, u32[]{:S(2)}, u32[]{:S(2)}) collective-permute-start(f32[864,128]{1,0:T(8,128)} %get-tuple-element.8), channel_id=1, source_target_pairs={{0,30},{1,31},{2,0},{3,1},{4,2},{5,3},{6,4},{7,5},{8,6},{9,7},{10,... | collective-permute-start | bytes 1327112 | tf_op jit(solution)/shard_map/ppermute | solution.py:180

commit v2 on v1

v2 whole, which is shorter than its diff:
```python
import math
import numpy as np
import jax
import jax.numpy as jnp
from jax import lax
from jax.sharding import PartitionSpec as P
from jax.experimental import pallas as pl
from jax.experimental.pallas import tpu as pltpu

mixing = 0.25
screening = 0.1
LANES = 128
F32 = jnp.float32
PAD = 8
LIMIT = 12 * 1024 * 1024


def split(values):
    values = np.asarray(values, np.float64)
    high = values.astype(jnp.bfloat16).astype(np.float64)
    low = (values - high).astype(jnp.bfloat16).astype(np.float64)
    return high.astype(np.float32), low.astype(np.float32)


def basis(extent):
    n, half = np.arange(extent), extent // 2
    rows = [np.full(extent, math.sqrt(1.0 / extent)), (1.0 - 2.0 * (n % 2)) * math.sqrt(1.0 / extent)]
    freqs = [0, half]
    for k in range(1, half):
        angle = 2.0 * math.pi * ((k * n) % extent) / extent
        rows += [math.sqrt(2.0 / extent) * np.cos(angle), math.sqrt(2.0 / extent) * np.sin(angle)]
        freqs += [k, k]
    return np.stack(rows), np.array(freqs)


def odd_basis(extent):
    n, rows, freqs = np.arange(extent), [], []
    for k in range(1, extent, 2):
        angle = math.pi * ((k * n) % (2 * extent)) / extent
        rows += [math.sqrt(2.0 / extent) * np.cos(angle), math.sqrt(2.0 / extent) * np.sin(angle)]
        freqs += [k, k]
    return np.stack(rows), np.array(freqs)


def lane_table(matrix):
    size = matrix.shape[0]
    table = np.zeros((2 * LANES, 2 * LANES), np.float32)
    for part in range(2):
        for col, values in enumerate(split(matrix)):
            table[part * LANES:part * LANES + size, col * LANES:col * LANES + size] = values
    return table


def row_table(matrix):
    high, low = split(matrix)
    return np.concatenate([high, high, low], axis=1)


def tables(extent):
    half = extent // 2
    full, freqs = basis(extent)
    even, even_freqs = basis(half)
    odd, odd_freqs = odd_basis(half)
    fold = np.array([[1.0, 1.0], [1.0, -1.0]]) / math.sqrt(2.0)
    square = lambda f: (2.0 * math.pi / extent * np.asarray(f, np.float64)) ** 2
    lanes = np.zeros((half, LANES))
    lanes[:, :extent] = square(2 * even_freqs)[:, None] + square(freqs)[None, :]
    lanes[:, extent:2 * extent] = square(odd_freqs)[:, None] + square(freqs)[None, :]
    kern = 1.0 / (square(np.arange(half + 1))[:, None, None] + lanes[None] + screening)
    return [jnp.asarray(t, F32) for t in (
        lane_table(np.kron(fold, full.T)), lane_table(np.kron(fold, full)),
        row_table(full), row_table(full.T),
        row_table(np.concatenate([even, odd])), row_table(np.concatenate([even.T, odd.T])), kern)]


def place_body(count, *refs):
    sems = refs[2 * count]
    copies = [pltpu.make_async_copy(refs[i], refs[count + i], sems.at[i]) for i in range(count)]
    for copy in copies:
        copy.start()
    for copy in copies:
        copy.wait()


def placed(*arrays):
    arrays = [pltpu.with_memory_space_constraint(a, pltpu.HBM) for a in arrays]
    return pl.pallas_call(
        lambda *refs: place_body(len(arrays), *refs),
        out_shape=[pltpu.VMEM(a.shape, F32) for a in arrays],
        in_specs=[pl.BlockSpec(memory_space=pltpu.HBM)] * len(arrays),
        out_specs=[pl.BlockSpec(memory_space=pltpu.VMEM)] * len(arrays),
        scratch_shapes=[pltpu.SemaphoreType.DMA((len(arrays),))],
        compiler_params=pltpu.CompilerParams(vmem_limit_bytes=LIMIT),
        name="place",
    )(*arrays)


def low_of(x):
    return x - x.astype(jnp.bfloat16).astype(F32)


def rows_apply(table, x):
    return jnp.dot(table, jnp.concatenate([x, low_of(x), x], axis=0), preferred_element_type=F32)


def lanes_apply(x, table):
    both = jnp.dot(jnp.concatenate([x, low_of(x)], axis=1), table, preferred_element_type=F32)
    return both[:, :LANES] + both[:, LANES:]


def beside(a, b):
    return jnp.concatenate([a, b], axis=1)


def pair_body(extent, adds, *refs):
    first_ref, prev_ref, fz_ref, iz_ref, fx_ref, ix_ref, fy_ref, iy_ref, kern_ref = refs[:9]
    if adds:
        weights_hbm, (more_ref, more_e_ref) = refs[9:12], refs[12:14]
        to_first_ref, to_prev_ref, e_ref, w_out_ref, t_ref, w_ref, sems = refs[14:]
        fetches = [pltpu.make_async_copy(weights_hbm[i], w_ref.at[i], sems.at[i]) for i in range(3)]
        for fetch in fetches:
            fetch.start()
    else:
        to_first_ref, to_prev_ref, e_ref, t_ref = refs[9:]
    half = extent // 2
    pitch = t_ref.shape[0] // half
    tiles = 3
    per = tiles * LANES // extent
    runs = extent // per
    row_stride = tiles * runs
    lane = lax.broadcasted_iota(jnp.int32, (extent, LANES), 1)
    low_half = lax.broadcasted_iota(jnp.int32, (half, 2 * LANES), 1) % LANES < extent
    fx, ix, fy, iy = fx_ref[...], ix_ref[...], fy_ref[...], iy_ref[...]

    def dense(ref, y1, t):
        return ref[pl.ds(tiles * y1 + t, extent, stride=row_stride), :]

    def pick(parts, start):
        t, off = divmod(start, LANES)
        if off + extent <= LANES:
            return parts[t], off
        return jnp.where(lane >= off, parts[t], parts[t + 1]), off

    def turn(x, shift):
        shift %= LANES
        return x if shift == 0 else pltpu.roll(x, shift, 1)

    for y1 in range(runs // 2):
        parts = [[dense(first_ref, y1 + h * (runs // 2), t) * dense(prev_ref, y1 + h * (runs // 2), t)
                  for t in range(tiles)] for h in range(2)]
        rows = []
        for y0 in range(per):
            a, off = pick(parts[0], y0 * extent)
            b, _ = pick(parts[1], y0 * extent)
            rows.append(jnp.where(lane < extent, turn(a, -off), turn(b, extent - off)))
        after = lanes_apply(jnp.concatenate(rows, axis=0), fz_ref[...])
        for y0 in range(0, per, 2):
            out = rows_apply(fx, beside(after[y0 * extent:(y0 + 1) * extent], after[(y0 + 1) * extent:(y0 + 2) * extent]))
            y = y1 * per + y0
            t_ref[pl.ds(y * pitch, extent), :] = out[:, :LANES]
            t_ref[pl.ds((y + 1) * pitch, extent), :] = out[:, LANES:]

    for p in range(half):
        at = [pl.ds(2 * p + i, half, stride=pitch) for i in range(2)]
        out = rows_apply(fy, beside(t_ref[at[0], :], t_ref[at[1], :]))
        ks = beside(kern_ref[0], kern_ref[half]) if p == 0 else beside(kern_ref[p], kern_ref[p])
        out = rows_apply(iy, jnp.where(low_half, out[:half], out[half:]) * ks)
        out = jnp.where(low_half, out[:half], out[half:])
        t_ref[at[0], :] = out[:, :LANES]
        t_ref[at[1], :] = out[:, LANES:]

    if adds:
        for fetch in fetches:
            fetch.wait()
        w_own, w_first, w_prev = (w_ref[i] for i in range(3))
    total = jnp.zeros((extent, LANES), F32)
    for y1 in range(runs // 2):
        rows = []
        for y0 in range(0, per, 2):
            y = y1 * per + y0
            out = rows_apply(ix, beside(t_ref[pl.ds(y * pitch, extent), :], t_ref[pl.ds((y + 1) * pitch, extent), :]))
            rows += [out[:, :LANES], out[:, LANES:]]
        after = lanes_apply(jnp.concatenate(rows, axis=0), iz_ref[...])
        pieces = [after[y0 * extent:(y0 + 1) * extent] for y0 in range(per)]
        for t in range(tiles):
            for h in range(2):
                v = None
                for y0 in range(per):
                    start = y0 * extent - t * LANES
                    if start < LANES and start + extent > 0:
                        piece = turn(pieces[y0], start - h * extent)
                        v = piece if v is None else jnp.where(lane >= start, piece, v)
                run = y1 + h * (runs // 2)
                prev, first = dense(prev_ref, run, t), dense(first_ref, run, t)
                at = pl.ds(tiles * run + t, extent, stride=row_stride)
                pv, fv = prev * v, first * v
                to_first_ref[at, :] = w_prev * pv if adds else pv
                to_prev_ref[at, :] = w_first * fv + w_own * more_ref[at, :] if adds else fv
                total = total + first * pv
    e_ref[...] = jnp.broadcast_to(jnp.sum(total), e_ref.shape)
    if adds:
        w_out_ref[...] = jnp.broadcast_to(w_prev, w_out_ref.shape)
        e_ref[...] = w_prev * (w_first * e_ref[...] + w_own * more_e_ref[...])


def pair_call(first, prev, constants, weights, more, count, name):
    rows = first.shape[0]
    extent = round((rows * LANES) ** (1.0 / 3.0))
    dense = jax.ShapeDtypeStruct((rows, LANES), F32)
    vm = pl.BlockSpec(memory_space=pltpu.VMEM)
    outs = [dense, dense, jax.ShapeDtypeStruct((count, LANES), F32)]
    if weights:
        outs.append(jax.ShapeDtypeStruct((1, LANES), F32))
    operands = [first, prev, *constants, *weights, *more]
    return pl.pallas_call(
        lambda *refs: pair_body(extent, 1 if more else 0, *refs),
        out_shape=outs,
        in_specs=[vm] * 9 + [pl.BlockSpec(memory_space=pl.ANY)] * len(weights) + [vm] * len(more),
        out_specs=[vm] * len(outs),
        scratch_shapes=[pltpu.VMEM((extent // 2 * (extent + PAD), LANES), F32)] + (
            [pltpu.VMEM((3, 1, 1), F32), pltpu.SemaphoreType.DMA((3,))] if weights else []),
        compiler_params=pltpu.CompilerParams(vmem_limit_bytes=LIMIT),
        name=name,
    )(*operands)


def combine_body(scale, e_scale, w_ref, mine_ref, back_ref, behind_ref, everyone_ref, out_ref, e_ref):
    out_ref[...] = scale * (w_ref[...] * mine_ref[...] + back_ref[...] + behind_ref[...])
    e_ref[...] = e_scale * jnp.sum(everyone_ref[...], axis=0, keepdims=True)[:, :1]


AXES = ("blk", "grp")


def moved(value, blocks, groups):
    n_blk, n_grp = lax.axis_size("blk"), lax.axis_size("grp")
    pairs = [(b * n_grp + g, (b + blocks) % n_blk * n_grp + (g + groups) % n_grp)
             for b in range(n_blk) for g in range(n_grp)]
    return lax.ppermute(value, AXES, pairs)


def local(orbitals, occupation):
    count = lax.axis_size(AXES)
    cells = orbitals.size
    weight = occupation.reshape(1, 1)
    own = orbitals.reshape(cells // LANES, LANES)
    previous, w_previous = moved(own, 1, 0), moved(weight, 1, 0)
    partner, w_partner = moved(own, 0, 1), moved(weight, 0, 1)
    mine_own, *constants = placed(own, *tables(round(cells ** (1.0 / 3.0))))
    mine, part, share = pair_call(mine_own, previous, constants, (), (), count, "own_pair")
    to_partner, to_previous, share, w_near = pair_call(
        partner, previous, constants, (weight, w_partner, w_previous), (part, share), count, "partner_pair")
    back = moved(to_partner, 0, 1)
    behind = moved(to_previous, -1, 0)
    everyone = lax.all_to_all(share, AXES, 0, 0, tiled=True)
    vm = pl.BlockSpec(memory_space=pltpu.VMEM)
    exchange, energy = pl.pallas_call(
        lambda *refs: combine_body(-mixing, -2.0 * mixing / (2.0 * cells * count), *refs),
        out_shape=(jax.ShapeDtypeStruct(own.shape, F32), jax.ShapeDtypeStruct((1, 1), F32)),
        in_specs=[vm] * 5, out_specs=(vm, vm),
        compiler_params=pltpu.CompilerParams(vmem_limit_bytes=LIMIT),
        name="combine",
    )(w_near, mine, back, behind, everyone)
    return exchange.reshape(orbitals.shape), energy.reshape(())


def solution(mesh):
    return jax.shard_map(local, mesh=mesh, in_specs=(P(AXES, None), P(AXES)),
                         out_specs=(P(AXES, None), P()), check_vma=False)
```

time: 41.8 us -> 33.4 us (0.80)
  waiting for transfers between devices: 8.2 us -> 4.74 us
  other arithmetic: 2.44 us -> 0 us
  between operations: 3.1 us -> 1.37 us
  Pallas kernels: 7.12 us -> 8.1 us
  local copies, waits for them, and re-layouts: 0.89 us -> 0 us
  blocking collectives: 9.76 us -> 9.22 us
    ppermute x6, waiting for transfers between devices: 8.2 us -> 4.74 us  [moved(): return lax.ppermute(value, AXES, pairs)]
    mul x1 -> x0, other arithmetic: 1.84 us -> none  [local(): exchange = (-mixing * (mine + back + behind)).reshape(1, cells)]
    pallas_call x1 -> x4, Pallas kernels: 7.12 us -> 8.1 us  [the longest x2 5.83 us: pair_call(): pl.pallas_call(lambda *refs: pair_body(extent, 1 if more else 0, *refs),...]
    unnamed x4 -> x0, local copies, waits for them, and re-layouts: 0.89 us -> none
    reduce_sum x1 -> x0, other arithmetic: 0.6 us -> none  [local(): jnp.sum(everyone[:, 0])]
    all_to_all x1, blocking collectives: 9.76 us -> 9.22 us  [local(): everyone = lax.all_to_all(share, AXES, 0, 0, tiled=True)]
  transfers between devices with their start and end apart: 6 -> 6, of which waited for: 1 -> 1; matrix products, arithmetic and copies ran while one was open for 1% -> 0% of each run, Pallas kernels for 0% -> 11%
where the time goes in v2:
time: 33.4 us; the launch traced here: 33.3 us
  starting transfers between devices  9.84 us (29%)
  blocking collectives  9.22 us (28%)
  Pallas kernels  8.1 us (24%)
  waiting for transfers between devices  4.74 us (14%)
  between operations  1.37 us (4%)
    ppermute x6, starting transfers between devices, moved(): return lax.ppermute(value, AXES, pairs)  9.84 us
    all_to_all x1, blocking collectives, local(): everyone = lax.all_to_all(share, AXES, 0, 0, tiled=True)  9.22 us
    pallas_call x2, Pallas kernels, pair_call(): pl.pallas_call(lambda *refs: pair_body(extent, 1 if more else 0, *refs),...  5.83 us
    ppermute x6, waiting for transfers between devices, moved(): return lax.ppermute(value, AXES, pairs)  4.74 us
    pallas_call x1, Pallas kernels, placed(): pl.pallas_call(lambda *refs: place_body(len(arrays), *refs), out_shape=[p...  1.4 us
    pallas_call x1, Pallas kernels, local(): pl.pallas_call(lambda *refs: combine_body(-mixing, -2.0 * mixing / (2.0 *...  0.87 us
  transfers between devices with their start and end apart: 6, of which 1 were waited for; matrix products, arithmetic and copies ran while one was open for 0% of the time, Pallas kernels for 11%

profile of v2, /device:TPU:0, one launch (start us, length us, event | category | flops | bytes accessed | tf_op | source)
XLA Modules:
  0.0 33.3 jit_solution(17333759435237381498)
XLA Ops:
  0.6 0.5 %collective-permute-start.1 = (f32[864,128]{1,0:T(8,128)}, f32[864,128]{1,0:T(8,128)S(1)}, u32[]{:S(2)}, u32[]{:S(2)}) collective-permute-start(f32[864,128]{1,0:T(8,128)} %bitcast.11), channel_id=1, source_target_pairs={{0,2},{1,3},{2,4},{3,5},{4,6},{5,7},{6,8},{7,9},{8,10},{9,11},{10,... | collective-permute-start | bytes 1327112 | tf_op jit(solution)/shard_map/ppermute | solution.py:239
  1.2 2.6 %collective-permute-start = (f32[864,128]{1,0:T(8,128)}, f32[864,128]{1,0:T(8,128)S(1)}, u32[]{:S(2)}, u32[]{:S(2)}) collective-permute-start(f32[864,128]{1,0:T(8,128)} %bitcast.12), channel_id=1, source_target_pairs={{0,1},{1,0},{2,3},{3,2},{4,5},{5,4},{6,7},{7,6},{8,9},{9,8},{10,11... | collective-permute-start | bytes 1327112 | tf_op jit(solution)/shard_map/ppermute | solution.py:239
  3.8 1.2 %collective-permute-start.3 = (f32[1,1]{1,0:T(1,128)}, f32[1,1]{1,0:T(1,128)}, u32[]{:S(2)}, u32[]{:S(2)}) collective-permute-start(f32[1,1]{1,0:T(1,128)} %bitcast.1), channel_id=1, source_target_pairs={{0,2},{1,3},{2,4},{3,5},{4,6},{5,7},{6,8},{7,9},{8,10},{9,11},{10,... | collective-permute-start | bytes 20 | tf_op jit(solution)/shard_map/ppermute | solution.py:239
  5.0 0.5 %collective-permute-start.2 = (f32[1,1]{1,0:T(1,128)}, f32[1,1]{1,0:T(1,128)}, u32[]{:S(2)}, u32[]{:S(2)}) collective-permute-start(f32[1,1]{1,0:T(1,128)} %bitcast.1), channel_id=1, source_target_pairs={{0,1},{1,0},{2,3},{3,2},{4,5},{5,4},{6,7},{7,6},{8,9},{9,8},{10,11... | collective-permute-start | bytes 20 | tf_op jit(solution)/shard_map/ppermute | solution.py:239
  6.2 1.4 %place.1 = (f32[864,128]{1,0:T(8,128)S(1)}, f32[256,256]{1,0:T(8,128)S(1)}, f32[256,256]{1,0:T(8,128)S(1)}, f32[48,144]{1,0:T(8,128)S(1)}, f32[48,144]{1,0:T(8,1...) custom-call(f32[864,128]{1,0:T(8,128)} %bitcast.13, ...), custom_call_target="tpu_custom_call" | custom-call | tf_op jit(solution)/shard_map/place/pallas_call | solution.py:87
  7.6 4.7 %collective-permute-done.1.refs_1_ = f32[864,128]{1,0:T(8,128)S(1)} collective-permute-done((f32[864,128]{1,0:T(8,128)}, f32[864,128]{1,0:T(8,128)S(1)}, u32[]{:S(2)}, u32[]{:S(2)}) %collective-permute-start.1) | collective-permute-done | bytes 442400 | tf_op jit(solution)/shard_map/ppermute | solution.py:239
  12.3 2.3 %own_pair.1 = (f32[864,128]{1,0:T(8,128)S(1)}, f32[864,128]{1,0:T(8,128)S(1)}, f32[32,128]{1,0:T(8,128)S(1)}) custom-call(f32[864,128]{1,0:T(8,128)S(1)} %get-tuple-element.26.refs_0_, f32[864,128]{1,0:T(8,128)S(1)} %collective-permute-done.1.refs_1_, f32[256,256]{1,0:T(8,128)S(1)} %get-tuple-element.19.refs_2_, f32[256,256]{1,0:T(8,128)S(1)} %get-tuple-element.20.refs_3_, ...), custom_call_target="tpu_custom_call" | custom-call | tf_op jit(solution)/shard_map/own_pair/pallas_call | solution.py:215
  14.6 0.0 collective-permute-done.3.refs_11_
  14.6 0.0 collective-permute-done.2.refs_10_
  14.6 0.0 collective-permute-done.refs_0_
  14.6 3.6 %partner_pair.1 = (f32[864,128]{1,0:T(8,128)S(1)}, f32[864,128]{1,0:T(8,128)S(1)}, f32[32,128]{1,0:T(8,128)S(1)}, f32[1,128]{1,0:T(1,128)S(1)}) custom-call(f32[864,128]{1,0:T(8,128)S(1)} %collective-permute-done.refs_0_, f32[864,128]{1,0:T(8,128)S(1)} %collective-permute-done.1.refs_1_, f32[256,256]{1,0:T(8,128)S(1)} %get-tuple-element.19.refs_2_, ...), custom_call_target="tpu_custom_call" | custom-call | tf_op jit(solution)/shard_map/partner_pair/pallas_call | solution.py:215
  18.2 2.1 %collective-permute-start.4 = (f32[864,128]{1,0:T(8,128)S(1)}, f32[864,128]{1,0:T(8,128)S(1)}, u32[]{:S(2)}, u32[]{:S(2)}) collective-permute-start(f32[864,128]{1,0:T(8,128)S(1)} %get-tuple-element.31), channel_id=1, source_target_pairs={{0,1},{1,0},{2,3},{3,2},{4,5},{5,4},{6,7},{7,6},{8,9},{9,8},{10,11... | collective-permute-start | bytes 1327112 | tf_op jit(solution)/shard_map/ppermute | solution.py:239
  20.2 2.9 %collective-permute-start.5 = (f32[864,128]{1,0:T(8,128)S(1)}, f32[864,128]{1,0:T(8,128)S(1)}, u32[]{:S(2)}, u32[]{:S(2)}) collective-permute-start(f32[864,128]{1,0:T(8,128)S(1)} %get-tuple-element.32), channel_id=1, source_target_pairs={{0,30},{1,31},{2,0},{3,1},{4,2},{5,3},{6,4},{7,5},{8,6},{9,7},{10,... | collective-permute-start | bytes 1327112 | tf_op jit(solution)/shard_map/ppermute | solution.py:239
  23.2 9.2 %all_to_all.11 = f32[32,1,128]{2,1,0:T(1,128)S(1)} all-to-all(f32[32,1,128]{2,1,0:T(1,128)S(1)} %bitcast.10), channel_id=1, replica_groups=mesh['blk'=16,'grp'=2] {'blk','grp'}, dimensions={0} | all-to-all | bytes 32768 | tf_op jit(solution)/shard_map/all_to_all | solution.py:255
  32.4 0.0 collective-permute-done.4.refs_2_
  32.4 0.0 collective-permute-done.5.refs_3_
  32.4 0.9 %combine.1 = (f32[864,128]{1,0:T(8,128)}, f32[1,1]{1,0:T(1,128)}) custom-call(f32[1,128]{1,0:T(1,128)S(1)} %get-tuple-element.29.refs_0_, f32[864,128]{1,0:T(8,128)S(1)} %get-tuple-element.30.refs_1_, f32[864,128]{1,0:T(8,128)S(1)} %collective-permute-done.4.refs_2_, f32[864,128]{1,0:T(8,128)S(1)} %collective-permute-done.5.refs_3_, f32[32,128]{1,0:T(8,128)S(1)} %bitcast.9), custom_call_target="tpu_custom_call" | custom-call | tf_op jit(solution)/shard_map/combine/pallas_call | solution.py:257
Async XLA Ops:
  0.6 11.7 %collective-permute-start.1 = (f32[864,128]{1,0:T(8,128)}, f32[864,128]{1,0:T(8,128)S(1)}, u32[]{:S(2)}, u32[]{:S(2)}) collective-permute-start(f32[864,128]{1,0:T(8,128)} %bitcast.11), channel_id=1, source_target_pairs={{0,2},{1,3},{2,4},{3,5},{4,6},{5,7},{6,8},{7,9},{8,10},{9,11},{10,... | collective-permute-start | bytes 1327112 | tf_op jit(solution)/shard_map/ppermute | solution.py:239
  1.2 13.4 %collective-permute-start = (f32[864,128]{1,0:T(8,128)}, f32[864,128]{1,0:T(8,128)S(1)}, u32[]{:S(2)}, u32[]{:S(2)}) collective-permute-start(f32[864,128]{1,0:T(8,128)} %bitcast.12), channel_id=1, source_target_pairs={{0,1},{1,0},{2,3},{3,2},{4,5},{5,4},{6,7},{7,6},{8,9},{9,8},{10,11... | collective-permute-start | bytes 1327112 | tf_op jit(solution)/shard_map/ppermute | solution.py:239
  3.8 10.8 %collective-permute-start.3 = (f32[1,1]{1,0:T(1,128)}, f32[1,1]{1,0:T(1,128)}, u32[]{:S(2)}, u32[]{:S(2)}) collective-permute-start(f32[1,1]{1,0:T(1,128)} %bitcast.1), channel_id=1, source_target_pairs={{0,2},{1,3},{2,4},{3,5},{4,6},{5,7},{6,8},{7,9},{8,10},{9,11},{10,... | collective-permute-start | bytes 20 | tf_op jit(solution)/shard_map/ppermute | solution.py:239
  5.0 9.6 %collective-permute-start.2 = (f32[1,1]{1,0:T(1,128)}, f32[1,1]{1,0:T(1,128)}, u32[]{:S(2)}, u32[]{:S(2)}) collective-permute-start(f32[1,1]{1,0:T(1,128)} %bitcast.1), channel_id=1, source_target_pairs={{0,1},{1,0},{2,3},{3,2},{4,5},{5,4},{6,7},{7,6},{8,9},{9,8},{10,11... | collective-permute-start | bytes 20 | tf_op jit(solution)/shard_map/ppermute | solution.py:239
  18.2 14.2 %collective-permute-start.4 = (f32[864,128]{1,0:T(8,128)S(1)}, f32[864,128]{1,0:T(8,128)S(1)}, u32[]{:S(2)}, u32[]{:S(2)}) collective-permute-start(f32[864,128]{1,0:T(8,128)S(1)} %get-tuple-element.31), channel_id=1, source_target_pairs={{0,1},{1,0},{2,3},{3,2},{4,5},{5,4},{6,7},{7,6},{8,9},{9,8},{10,11... | collective-permute-start | bytes 1327112 | tf_op jit(solution)/shard_map/ppermute | solution.py:239
  20.2 12.1 %collective-permute-start.5 = (f32[864,128]{1,0:T(8,128)S(1)}, f32[864,128]{1,0:T(8,128)S(1)}, u32[]{:S(2)}, u32[]{:S(2)}) collective-permute-start(f32[864,128]{1,0:T(8,128)S(1)} %get-tuple-element.32), channel_id=1, source_target_pairs={{0,30},{1,31},{2,0},{3,1},{4,2},{5,3},{6,4},{7,5},{8,6},{9,7},{10,... | collective-permute-start | bytes 1327112 | tf_op jit(solution)/shard_map/ppermute | solution.py:239

commit v3 on v2

--- a/solution.py
+++ b/solution.py
@@ -115,11 +115,8 @@
 def pair_body(extent, adds, *refs):
     first_ref, prev_ref, fz_ref, iz_ref, fx_ref, ix_ref, fy_ref, iy_ref, kern_ref = refs[:9]
     if adds:
-        weights_hbm, (more_ref, more_e_ref) = refs[9:12], refs[12:14]
-        to_first_ref, to_prev_ref, e_ref, w_out_ref, t_ref, w_ref, sems = refs[14:]
-        fetches = [pltpu.make_async_copy(weights_hbm[i], w_ref.at[i], sems.at[i]) for i in range(3)]
-        for fetch in fetches:
-            fetch.start()
+        w_refs, (more_ref, more_e_ref) = refs[9:12], refs[12:14]
+        to_first_ref, to_prev_ref, e_ref, t_ref = refs[14:]
     else:
         to_first_ref, to_prev_ref, e_ref, t_ref = refs[9:]
     half = extent // 2
@@ -170,9 +167,7 @@
         t_ref[at[1], :] = out[:, LANES:]
 
     if adds:
-        for fetch in fetches:
-            fetch.wait()
-        w_own, w_first, w_prev = (w_ref[i] for i in range(3))
+        w_own, w_first, w_prev = (w_ref[:1, :] for w_ref in w_refs)
     total = jnp.zeros((extent, LANES), F32)
     for y1 in range(runs // 2):
         rows = []
@@ -199,7 +194,6 @@
                 total = total + first * pv
     e_ref[...] = jnp.broadcast_to(jnp.sum(total), e_ref.shape)
     if adds:
-        w_out_ref[...] = jnp.broadcast_to(w_prev, w_out_ref.shape)
         e_ref[...] = w_prev * (w_first * e_ref[...] + w_own * more_e_ref[...])
 
 
@@ -209,23 +203,20 @@
     dense = jax.ShapeDtypeStruct((rows, LANES), F32)
     vm = pl.BlockSpec(memory_space=pltpu.VMEM)
     outs = [dense, dense, jax.ShapeDtypeStruct((count, LANES), F32)]
-    if weights:
-        outs.append(jax.ShapeDtypeStruct((1, LANES), F32))
     operands = [first, prev, *constants, *weights, *more]
     return pl.pallas_call(
         lambda *refs: pair_body(extent, 1 if more else 0, *refs),
         out_shape=outs,
-        in_specs=[vm] * 9 + [pl.BlockSpec(memory_space=pl.ANY)] * len(weights) + [vm] * len(more),
+        in_specs=[vm] * len(operands),
         out_specs=[vm] * len(outs),
-        scratch_shapes=[pltpu.VMEM((extent // 2 * (extent + PAD), LANES), F32)] + (
-            [pltpu.VMEM((3, 1, 1), F32), pltpu.SemaphoreType.DMA((3,))] if weights else []),
+        scratch_shapes=[pltpu.VMEM((extent // 2 * (extent + PAD), LANES), F32)],
         compiler_params=pltpu.CompilerParams(vmem_limit_bytes=LIMIT),
         name=name,
     )(*operands)
 
 
 def combine_body(scale, e_scale, w_ref, mine_ref, back_ref, behind_ref, everyone_ref, out_ref, e_ref):
-    out_ref[...] = scale * (w_ref[...] * mine_ref[...] + back_ref[...] + behind_ref[...])
+    out_ref[...] = scale * (w_ref[:1, :] * mine_ref[...] + back_ref[...] + behind_ref[...])
     e_ref[...] = e_scale * jnp.sum(everyone_ref[...], axis=0, keepdims=True)[:, :1]
 
 
@@ -242,13 +233,13 @@
 def local(orbitals, occupation):
     count = lax.axis_size(AXES)
     cells = orbitals.size
-    weight = occupation.reshape(1, 1)
+    weight = jnp.broadcast_to(occupation[:, None], (8, LANES))
     own = orbitals.reshape(cells // LANES, LANES)
     previous, w_previous = moved(own, 1, 0), moved(weight, 1, 0)
     partner, w_partner = moved(own, 0, 1), moved(weight, 0, 1)
     mine_own, *constants = placed(own, *tables(round(cells ** (1.0 / 3.0))))
     mine, part, share = pair_call(mine_own, previous, constants, (), (), count, "own_pair")
-    to_partner, to_previous, share, w_near = pair_call(
+    to_partner, to_previous, share = pair_call(
         partner, previous, constants, (weight, w_partner, w_previous), (part, share), count, "partner_pair")
     back = moved(to_partner, 0, 1)
     behind = moved(to_previous, -1, 0)
@@ -260,7 +251,7 @@
         in_specs=[vm] * 5, out_specs=(vm, vm),
         compiler_params=pltpu.CompilerParams(vmem_limit_bytes=LIMIT),
         name="combine",
-    )(w_near, mine, back, behind, everyone)
+    )(w_previous, mine, back, behind, everyone)
     return exchange.reshape(orbitals.shape), energy.reshape(())
 
 

time: 33.4 us -> 32.1 us (0.961)
  Pallas kernels: 8.1 us -> 6.84 us
    pallas_call x2, Pallas kernels: 5.83 us -> 4.54 us  [pair_call(): pl.pallas_call(lambda *refs: pair_body(extent, 1 if more else 0, *refs),...]
where the time goes in v3:
time: 32.1 us; the launch traced here: 32 us
  starting transfers between devices  9.95 us (31%)
  blocking collectives  9.12 us (28%)
  Pallas kernels  6.84 us (21%)
  waiting for transfers between devices  4.72 us (15%)
  between operations  1.34 us (4%)
    ppermute x6, starting transfers between devices, moved(): return lax.ppermute(value, AXES, pairs)  9.95 us
    all_to_all x1, blocking collectives, local(): everyone = lax.all_to_all(share, AXES, 0, 0, tiled=True)  9.12 us
    ppermute x6, waiting for transfers between devices, moved(): return lax.ppermute(value, AXES, pairs)  4.72 us
    pallas_call x2, Pallas kernels, pair_call(): pl.pallas_call(lambda *refs: pair_body(extent, 1 if more else 0, *refs),...  4.54 us
    pallas_call x1, Pallas kernels, placed(): pl.pallas_call(lambda *refs: place_body(len(arrays), *refs), out_shape=[p...  1.39 us
    pallas_call x1, Pallas kernels, local(): pl.pallas_call(lambda *refs: combine_body(-mixing, -2.0 * mixing / (2.0 *...  0.91 us
  transfers between devices with their start and end apart: 6, of which 1 were waited for; matrix products, arithmetic and copies ran while one was open for 0% of the time, Pallas kernels for 11%

profile of v3, /device:TPU:0, one launch (start us, length us, event | category | flops | bytes accessed | tf_op | source)
XLA Modules:
  0.0 32.0 jit_solution(4209337287603568162)
XLA Ops:
  0.6 0.5 %collective-permute-start.1 = (f32[864,128]{1,0:T(8,128)}, f32[864,128]{1,0:T(8,128)S(1)}, u32[]{:S(2)}, u32[]{:S(2)}) collective-permute-start(f32[864,128]{1,0:T(8,128)} %bitcast.11), channel_id=1, source_target_pairs={{0,2},{1,3},{2,4},{3,5},{4,6},{5,7},{6,8},{7,9},{8,10},{9,11},{10,... | collective-permute-start | bytes 1327112 | tf_op jit(solution)/shard_map/ppermute | solution.py:230
  1.2 2.6 %collective-permute-start.2 = (f32[864,128]{1,0:T(8,128)}, f32[864,128]{1,0:T(8,128)S(1)}, u32[]{:S(2)}, u32[]{:S(2)}) collective-permute-start(f32[864,128]{1,0:T(8,128)} %bitcast.12), channel_id=1, source_target_pairs={{0,1},{1,0},{2,3},{3,2},{4,5},{5,4},{6,7},{7,6},{8,9},{9,8},{10,11... | collective-permute-start | bytes 1327112 | tf_op jit(solution)/shard_map/ppermute | solution.py:230
  4.4 1.3 %collective-permute-start = (f32[8,128]{1,0:T(8,128)S(1)}, f32[8,128]{1,0:T(8,128)S(1)}, u32[]{:S(2)}, u32[]{:S(2)}) collective-permute-start(f32[8,128]{1,0:T(8,128)S(1)} %broadcast_in_dim.9.refs_9_), channel_id=1, source_target_pairs={{0,2},{1,3},{2,4},{3,5},{4,6},{5,7},{6,8},{7,9},{8,10},{9,11},{10,... | collective-permute-start | bytes 12296 | tf_op jit(solution)/shard_map/ppermute | solution.py:230
  5.7 0.5 %collective-permute-start.3 = (f32[8,128]{1,0:T(8,128)S(1)}, f32[8,128]{1,0:T(8,128)S(1)}, u32[]{:S(2)}, u32[]{:S(2)}) collective-permute-start(f32[8,128]{1,0:T(8,128)S(1)} %broadcast_in_dim.9.refs_9_), channel_id=1, source_target_pairs={{0,1},{1,0},{2,3},{3,2},{4,5},{5,4},{6,7},{7,6},{8,9},{9,8},{10,11... | collective-permute-start | bytes 12296 | tf_op jit(solution)/shard_map/ppermute | solution.py:230
  6.2 1.4 %place.1 = (f32[864,128]{1,0:T(8,128)S(1)}, f32[256,256]{1,0:T(8,128)S(1)}, f32[256,256]{1,0:T(8,128)S(1)}, f32[48,144]{1,0:T(8,128)S(1)}, f32[48,144]{1,0:T(8,1...) custom-call(f32[864,128]{1,0:T(8,128)} %bitcast.13, ...), custom_call_target="tpu_custom_call" | custom-call | tf_op jit(solution)/shard_map/place/pallas_call | solution.py:87
  7.6 4.7 %collective-permute-done.1.refs_1_ = f32[864,128]{1,0:T(8,128)S(1)} collective-permute-done((f32[864,128]{1,0:T(8,128)}, f32[864,128]{1,0:T(8,128)S(1)}, u32[]{:S(2)}, u32[]{:S(2)}) %collective-permute-start.1) | collective-permute-done | bytes 442400 | tf_op jit(solution)/shard_map/ppermute | solution.py:230
  12.3 2.3 %own_pair.1 = (f32[864,128]{1,0:T(8,128)S(1)}, f32[864,128]{1,0:T(8,128)S(1)}, f32[32,128]{1,0:T(8,128)S(1)}) custom-call(f32[864,128]{1,0:T(8,128)S(1)} %get-tuple-element.18.refs_0_, f32[864,128]{1,0:T(8,128)S(1)} %collective-permute-done.1.refs_1_, f32[256,256]{1,0:T(8,128)S(1)} %get-tuple-element.19.refs_2_, f32[256,256]{1,0:T(8,128)S(1)} %get-tuple-element.20.refs_3_, ...), custom_call_target="tpu_custom_call" | custom-call | tf_op jit(solution)/shard_map/own_pair/pallas_call | solution.py:207
  14.6 0.0 collective-permute-done.refs_11_.refs_0_
  14.6 0.0 collective-permute-done.3.refs_10_
  14.6 0.0 collective-permute-done.2.refs_0_
  14.6 2.3 %partner_pair.1 = (f32[864,128]{1,0:T(8,128)S(1)}, f32[864,128]{1,0:T(8,128)S(1)}, f32[32,128]{1,0:T(8,128)S(1)}) custom-call(f32[864,128]{1,0:T(8,128)S(1)} %collective-permute-done.2.refs_0_, f32[864,128]{1,0:T(8,128)S(1)} %collective-permute-done.1.refs_1_, f32[256,256]{1,0:T(8,128)S(1)} %get-tuple-element.19.refs_2_, ...), custom_call_target="tpu_custom_call" | custom-call | tf_op jit(solution)/shard_map/partner_pair/pallas_call | solution.py:207
  16.9 2.0 %collective-permute-start.4 = (f32[864,128]{1,0:T(8,128)S(1)}, f32[864,128]{1,0:T(8,128)S(1)}, u32[]{:S(2)}, u32[]{:S(2)}) collective-permute-start(f32[864,128]{1,0:T(8,128)S(1)} %get-tuple-element.29), channel_id=1, source_target_pairs={{0,1},{1,0},{2,3},{3,2},{4,5},{5,4},{6,7},{7,6},{8,9},{9,8},{10,11... | collective-permute-start | bytes 1327112 | tf_op jit(solution)/shard_map/ppermute | solution.py:230
  19.0 3.0 %collective-permute-start.5 = (f32[864,128]{1,0:T(8,128)S(1)}, f32[864,128]{1,0:T(8,128)S(1)}, u32[]{:S(2)}, u32[]{:S(2)}) collective-permute-start(f32[864,128]{1,0:T(8,128)S(1)} %get-tuple-element.30), channel_id=1, source_target_pairs={{0,30},{1,31},{2,0},{3,1},{4,2},{5,3},{6,4},{7,5},{8,6},{9,7},{10,... | collective-permute-start | bytes 1327112 | tf_op jit(solution)/shard_map/ppermute | solution.py:230
  21.9 9.1 %all_to_all.11 = f32[32,1,128]{2,1,0:T(1,128)S(1)} all-to-all(f32[32,1,128]{2,1,0:T(1,128)S(1)} %bitcast.10), channel_id=1, replica_groups=mesh['blk'=16,'grp'=2] {'blk','grp'}, dimensions={0} | all-to-all | bytes 32768 | tf_op jit(solution)/shard_map/all_to_all | solution.py:246
  31.0 0.0 collective-permute-done.4.refs_2_
  31.1 0.0 collective-permute-done.5.refs_3_
  31.1 0.9 %combine.1 = (f32[864,128]{1,0:T(8,128)}, f32[1,1]{1,0:T(1,128)}) custom-call(f32[8,128]{1,0:T(8,128)S(1)} %collective-permute-done.refs_11_.refs_0_, f32[864,128]{1,0:T(8,128)S(1)} %get-tuple-element.26.refs_1_, f32[864,128]{1,0:T(8,128)S(1)} %collective-permute-done.4.refs_2_, f32[864,128]{1,0:T(8,128)S(1)} %collective-permute-done.5.refs_3_, ...), custom_call_target="tpu_custom_call" | custom-call | tf_op jit(solution)/shard_map/combine/pallas_call | solution.py:248
  (1 shorter events, 0.0 us)
Async XLA Ops:
  0.6 11.7 %collective-permute-start.1 = (f32[864,128]{1,0:T(8,128)}, f32[864,128]{1,0:T(8,128)S(1)}, u32[]{:S(2)}, u32[]{:S(2)}) collective-permute-start(f32[864,128]{1,0:T(8,128)} %bitcast.11), channel_id=1, source_target_pairs={{0,2},{1,3},{2,4},{3,5},{4,6},{5,7},{6,8},{7,9},{8,10},{9,11},{10,... | collective-permute-start | bytes 1327112 | tf_op jit(solution)/shard_map/ppermute | solution.py:230
  1.2 13.4 %collective-permute-start.2 = (f32[864,128]{1,0:T(8,128)}, f32[864,128]{1,0:T(8,128)S(1)}, u32[]{:S(2)}, u32[]{:S(2)}) collective-permute-start(f32[864,128]{1,0:T(8,128)} %bitcast.12), channel_id=1, source_target_pairs={{0,1},{1,0},{2,3},{3,2},{4,5},{5,4},{6,7},{7,6},{8,9},{9,8},{10,11... | collective-permute-start | bytes 1327112 | tf_op jit(solution)/shard_map/ppermute | solution.py:230
  4.4 10.2 %collective-permute-start = (f32[8,128]{1,0:T(8,128)S(1)}, f32[8,128]{1,0:T(8,128)S(1)}, u32[]{:S(2)}, u32[]{:S(2)}) collective-permute-start(f32[8,128]{1,0:T(8,128)S(1)} %broadcast_in_dim.9.refs_9_), channel_id=1, source_target_pairs={{0,2},{1,3},{2,4},{3,5},{4,6},{5,7},{6,8},{7,9},{8,10},{9,11},{10,... | collective-permute-start | bytes 12296 | tf_op jit(solution)/shard_map/ppermute | solution.py:230
  5.7 8.9 %collective-permute-start.3 = (f32[8,128]{1,0:T(8,128)S(1)}, f32[8,128]{1,0:T(8,128)S(1)}, u32[]{:S(2)}, u32[]{:S(2)}) collective-permute-start(f32[8,128]{1,0:T(8,128)S(1)} %broadcast_in_dim.9.refs_9_), channel_id=1, source_target_pairs={{0,1},{1,0},{2,3},{3,2},{4,5},{5,4},{6,7},{7,6},{8,9},{9,8},{10,11... | collective-permute-start | bytes 12296 | tf_op jit(solution)/shard_map/ppermute | solution.py:230
  16.9 14.1 %collective-permute-start.4 = (f32[864,128]{1,0:T(8,128)S(1)}, f32[864,128]{1,0:T(8,128)S(1)}, u32[]{:S(2)}, u32[]{:S(2)}) collective-permute-start(f32[864,128]{1,0:T(8,128)S(1)} %get-tuple-element.29), channel_id=1, source_target_pairs={{0,1},{1,0},{2,3},{3,2},{4,5},{5,4},{6,7},{7,6},{8,9},{9,8},{10,11... | collective-permute-start | bytes 1327112 | tf_op jit(solution)/shard_map/ppermute | solution.py:230
  19.0 12.1 %collective-permute-start.5 = (f32[864,128]{1,0:T(8,128)S(1)}, f32[864,128]{1,0:T(8,128)S(1)}, u32[]{:S(2)}, u32[]{:S(2)}) collective-permute-start(f32[864,128]{1,0:T(8,128)S(1)} %get-tuple-element.30), channel_id=1, source_target_pairs={{0,30},{1,31},{2,0},{3,1},{4,2},{5,3},{6,4},{7,5},{8,6},{9,7},{10,... | collective-permute-start | bytes 1327112 | tf_op jit(solution)/shard_map/ppermute | solution.py:230

commit v4 on v3

--- a/solution.py
+++ b/solution.py
@@ -6,6 +6,7 @@
 from jax.sharding import PartitionSpec as P
 from jax.experimental import pallas as pl
 from jax.experimental.pallas import tpu as pltpu
+
 
 mixing = 0.25
 screening = 0.1
@@ -68,25 +69,33 @@
     lanes[:, extent:2 * extent] = square(odd_freqs)[:, None] + square(freqs)[None, :]
     kern = 1.0 / (square(np.arange(half + 1))[:, None, None] + lanes[None] + screening)
     return [jnp.asarray(t, F32) for t in (
-        lane_table(np.kron(fold, full.T)), lane_table(np.kron(fold, full)),
-        row_table(full), row_table(full.T),
-        row_table(np.concatenate([even, odd])), row_table(np.concatenate([even.T, odd.T])), kern)]
-
-
-def place_body(count, *refs):
+        lane_table(np.kron(fold, full.T)), row_table(full), row_table(full.T),
+        row_table(np.concatenate([even, odd])), row_table(np.concatenate([even.T, odd.T])), kern,
+        lane_table(np.kron(fold, full)))]
+
+
+def place_body(count, variants, *refs):
     sems = refs[2 * count]
-    copies = [pltpu.make_async_copy(refs[i], refs[count + i], sems.at[i]) for i in range(count)]
-    for copy in copies:
+    rolled_ref = refs[2 * count - 1]
+    targets = [*refs[count:2 * count - 1], rolled_ref.at[0]]
+    copies = [pltpu.make_async_copy(refs[i], targets[i], sems.at[i]) for i in range(count)]
+    for copy in copies[::-1]:
         copy.start()
-    for copy in copies:
+    copies[-1].wait()
+    for i in range(1, len(variants)):
+        for at in range(0, rolled_ref.shape[2], LANES):
+            rolled_ref[i, :, at:at + LANES] = pltpu.roll(rolled_ref[0, :, at:at + LANES], variants[i], 1)
+    for copy in copies[:-1]:
         copy.wait()
 
 
-def placed(*arrays):
+def placed(variants, *arrays):
     arrays = [pltpu.with_memory_space_constraint(a, pltpu.HBM) for a in arrays]
+    shapes = [a.shape for a in arrays]
+    shapes[-1] = (len(variants), *shapes[-1])
     return pl.pallas_call(
-        lambda *refs: place_body(len(arrays), *refs),
-        out_shape=[pltpu.VMEM(a.shape, F32) for a in arrays],
+        lambda *refs: place_body(len(arrays), variants, *refs),
+        out_shape=[pltpu.VMEM(s, F32) for s in shapes],
         in_specs=[pl.BlockSpec(memory_space=pltpu.HBM)] * len(arrays),
         out_specs=[pl.BlockSpec(memory_space=pltpu.VMEM)] * len(arrays),
         scratch_shapes=[pltpu.SemaphoreType.DMA((len(arrays),))],
@@ -113,7 +122,7 @@
 
 
 def pair_body(extent, adds, *refs):
-    first_ref, prev_ref, fz_ref, iz_ref, fx_ref, ix_ref, fy_ref, iy_ref, kern_ref = refs[:9]
+    first_ref, prev_ref, fz_ref, fx_ref, ix_ref, fy_ref, iy_ref, kern_ref, iz_ref = refs[:9]
     if adds:
         w_refs, (more_ref, more_e_ref) = refs[9:12], refs[12:14]
         to_first_ref, to_prev_ref, e_ref, t_ref = refs[14:]
@@ -121,7 +130,7 @@
         to_first_ref, to_prev_ref, e_ref, t_ref = refs[9:]
     half = extent // 2
     pitch = t_ref.shape[0] // half
-    tiles = 3
+    tiles = math.lcm(extent, LANES) // LANES
     per = tiles * LANES // extent
     runs = extent // per
     row_stride = tiles * runs
@@ -132,30 +141,46 @@
     def dense(ref, y1, t):
         return ref[pl.ds(tiles * y1 + t, extent, stride=row_stride), :]
 
-    def pick(parts, start):
-        t, off = divmod(start, LANES)
+    def row(parts, y0):
+        t, off = divmod(y0 * extent, LANES)
         if off + extent <= LANES:
-            return parts[t], off
-        return jnp.where(lane >= off, parts[t], parts[t + 1]), off
-
-    def turn(x, shift):
-        shift %= LANES
-        return x if shift == 0 else pltpu.roll(x, shift, 1)
-
-    for y1 in range(runs // 2):
-        parts = [[dense(first_ref, y1 + h * (runs // 2), t) * dense(prev_ref, y1 + h * (runs // 2), t)
-                  for t in range(tiles)] for h in range(2)]
-        rows = []
-        for y0 in range(per):
-            a, off = pick(parts[0], y0 * extent)
-            b, _ = pick(parts[1], y0 * extent)
-            rows.append(jnp.where(lane < extent, turn(a, -off), turn(b, extent - off)))
-        after = lanes_apply(jnp.concatenate(rows, axis=0), fz_ref[...])
-        for y0 in range(0, per, 2):
-            out = rows_apply(fx, beside(after[y0 * extent:(y0 + 1) * extent], after[(y0 + 1) * extent:(y0 + 2) * extent]))
-            y = y1 * per + y0
-            t_ref[pl.ds(y * pitch, extent), :] = out[:, :LANES]
-            t_ref[pl.ds((y + 1) * pitch, extent), :] = out[:, LANES:]
+            a, b = parts[0][t], parts[1][t]
+            inside = lane < off + extent
+            if off + 2 * extent > LANES:
+                inside &= lane >= off
+            return jnp.where(inside, a, b)
+        a = jnp.where(lane >= off, parts[0][t], parts[0][t + 1])
+        b = jnp.where(lane < extent, parts[1][t], parts[1][t + 1])
+        return jnp.where((lane >= off + extent - LANES) & (lane < off), b, a)
+
+    def turned_table(off):
+        if off == 0:
+            return fz_ref[...]
+        cuts = [fz_ref[at + s:at + e] for at in (0, LANES) for s, e in ((LANES - off, LANES), (0, LANES - off))]
+        return jnp.concatenate(cuts, axis=0)
+
+    steps = runs // 2
+    parts = []
+    for y1 in range(steps):
+        both = [[dense(first_ref, y1 + h * steps, t) * dense(prev_ref, y1 + h * steps, t)
+                 for t in range(tiles)] for h in range(2)]
+        parts.append([both[0], [pltpu.roll(p, extent, 1) for p in both[1]]])
+
+    def rows_of(y):
+        return pl.ds(y * pitch, extent)
+
+    def along_rows(table):
+        for y in range(0, half, 2):
+            out = rows_apply(table, beside(t_ref[rows_of(y), :], t_ref[rows_of(y + 1), :]))
+            t_ref[rows_of(y), :] = out[:, :LANES]
+            t_ref[rows_of(y + 1), :] = out[:, LANES:]
+
+    for y0 in range(per):
+        after = lanes_apply(jnp.concatenate([row(parts[y1], y0) for y1 in range(steps)], axis=0),
+                            turned_table(y0 * extent % LANES))
+        for y1 in range(steps):
+            t_ref[rows_of(y1 * per + y0), :] = after[y1 * extent:(y1 + 1) * extent]
+    along_rows(fx)
 
     for p in range(half):
         at = [pl.ds(2 * p + i, half, stride=pitch) for i in range(2)]
@@ -169,35 +194,43 @@
     if adds:
         w_own, w_first, w_prev = (w_ref[:1, :] for w_ref in w_refs)
     total = jnp.zeros((extent, LANES), F32)
-    for y1 in range(runs // 2):
-        rows = []
-        for y0 in range(0, per, 2):
-            y = y1 * per + y0
-            out = rows_apply(ix, beside(t_ref[pl.ds(y * pitch, extent), :], t_ref[pl.ds((y + 1) * pitch, extent), :]))
-            rows += [out[:, :LANES], out[:, LANES:]]
-        after = lanes_apply(jnp.concatenate(rows, axis=0), iz_ref[...])
-        pieces = [after[y0 * extent:(y0 + 1) * extent] for y0 in range(per)]
-        for t in range(tiles):
+    turned_lane = (lane + LANES - extent) % LANES
+    tile_of = {}
+
+    def finish(t):
+        nonlocal total
+        for y1 in range(steps):
             for h in range(2):
-                v = None
-                for y0 in range(per):
-                    start = y0 * extent - t * LANES
-                    if start < LANES and start + extent > 0:
-                        piece = turn(pieces[y0], start - h * extent)
-                        v = piece if v is None else jnp.where(lane >= start, piece, v)
-                run = y1 + h * (runs // 2)
+                v = tile_of.pop((t, y1, h))
+                if h:
+                    v = pltpu.roll(v, LANES - extent, 1)
+                run = y1 + h * steps
                 prev, first = dense(prev_ref, run, t), dense(first_ref, run, t)
                 at = pl.ds(tiles * run + t, extent, stride=row_stride)
                 pv, fv = prev * v, first * v
                 to_first_ref[at, :] = w_prev * pv if adds else pv
                 to_prev_ref[at, :] = w_first * fv + w_own * more_ref[at, :] if adds else fv
                 total = total + first * pv
+
+    along_rows(ix)
+    for y0 in range(per):
+        start = y0 * extent
+        after = lanes_apply(jnp.concatenate([t_ref[rows_of(y1 * per + y0), :] for y1 in range(steps)], axis=0), iz_ref[y0])
+        for t in range(start // LANES, (start + extent - 1) // LANES + 1):
+            for y1 in range(steps):
+                piece = after[y1 * extent:(y1 + 1) * extent]
+                for h in range(2):
+                    held = tile_of.get((t, y1, h))
+                    where = turned_lane if h else lane
+                    tile_of[t, y1, h] = piece if held is None else jnp.where(where >= start - t * LANES, piece, held)
+        if (start + extent) // LANES > start // LANES:
+            finish(start // LANES)
     e_ref[...] = jnp.broadcast_to(jnp.sum(total), e_ref.shape)
     if adds:
         e_ref[...] = w_prev * (w_first * e_ref[...] + w_own * more_e_ref[...])
 
 
-def pair_call(first, prev, constants, weights, more, count, name):
+def pair_call(first, prev, constants, weights, more, count):
     rows = first.shape[0]
     extent = round((rows * LANES) ** (1.0 / 3.0))
     dense = jax.ShapeDtypeStruct((rows, LANES), F32)
@@ -211,7 +244,6 @@
         out_specs=[vm] * len(outs),
         scratch_shapes=[pltpu.VMEM((extent // 2 * (extent + PAD), LANES), F32)],
         compiler_params=pltpu.CompilerParams(vmem_limit_bytes=LIMIT),
-        name=name,
     )(*operands)
 
 
@@ -235,12 +267,15 @@
     cells = orbitals.size
     weight = jnp.broadcast_to(occupation[:, None], (8, LANES))
     own = orbitals.reshape(cells // LANES, LANES)
-    previous, w_previous = moved(own, 1, 0), moved(weight, 1, 0)
-    partner, w_partner = moved(own, 0, 1), moved(weight, 0, 1)
-    mine_own, *constants = placed(own, *tables(round(cells ** (1.0 / 3.0))))
-    mine, part, share = pair_call(mine_own, previous, constants, (), (), count, "own_pair")
+    partner = moved(own, 0, 1)
+    previous = moved(own, 1, 0)
+    w_partner, w_previous = moved(weight, 0, 1), moved(weight, 1, 0)
+    extent = round(cells ** (1.0 / 3.0))
+    variants = [y0 * extent % LANES for y0 in range(math.lcm(extent, LANES) // extent)]
+    mine_own, *constants = placed(variants, own, *tables(extent))
+    mine, part, share = pair_call(mine_own, previous, constants, (), (), count)
     to_partner, to_previous, share = pair_call(
-        partner, previous, constants, (weight, w_partner, w_previous), (part, share), count, "partner_pair")
+        partner, previous, constants, (weight, w_partner, w_previous), (part, share), count)
     back = moved(to_partner, 0, 1)
     behind = moved(to_previous, -1, 0)
     everyone = lax.all_to_all(share, AXES, 0, 0, tiled=True)

time: 32.1 us -> 31.7 us (0.988)
  Pallas kernels: 6.84 us -> 6.2 us
  starting transfers between devices: 9.95 us -> 10.4 us
    pallas_call x2, Pallas kernels: 4.54 us -> 3.72 us  [pair_call(): pl.pallas_call(lambda *refs: pair_body(extent, 1 if more else 0, *refs),...]
    ppermute x6, starting transfers between devices: 9.95 us -> 10.4 us  [moved(): return lax.ppermute(value, AXES, pairs)]
where the time goes in v4:
time: 31.7 us; the launch traced here: 31.6 us
  starting transfers between devices  10.4 us (33%)
  blocking collectives  9.12 us (29%)
  Pallas kernels  6.2 us (20%)
  waiting for transfers between devices  4.54 us (14%)
  between operations  1.34 us (4%)
    ppermute x6, starting transfers between devices, moved(): return lax.ppermute(value, AXES, pairs)  10.4 us
    all_to_all x1, blocking collectives, local(): everyone = lax.all_to_all(share, AXES, 0, 0, tiled=True)  9.12 us
    ppermute x6, waiting for transfers between devices, moved(): return lax.ppermute(value, AXES, pairs)  4.54 us
    pallas_call x2, Pallas kernels, pair_call(): pl.pallas_call(lambda *refs: pair_body(extent, 1 if more else 0, *refs),...  3.72 us
    pallas_call x1, Pallas kernels, placed(): pl.pallas_call(lambda *refs: place_body(len(arrays), variants, *refs), ou...  1.57 us
    pallas_call x1, Pallas kernels, local(): pl.pallas_call(lambda *refs: combine_body(-mixing, -2.0 * mixing / (2.0 *...  0.91 us
  transfers between devices with their start and end apart: 6, of which 1 were waited for; matrix products, arithmetic and copies ran while one was open for 0% of the time, Pallas kernels for 11%

profile of v4, /device:TPU:0, one launch (start us, length us, event | category | flops | bytes accessed | tf_op | source)
XLA Modules:
  0.0 31.6 jit_solution(18402010257809870255)
XLA Ops:
  0.6 0.5 %collective-permute-start.1 = (f32[864,128]{1,0:T(8,128)}, f32[864,128]{1,0:T(8,128)S(1)}, u32[]{:S(2)}, u32[]{:S(2)}) collective-permute-start(f32[864,128]{1,0:T(8,128)} %bitcast.11), channel_id=1, source_target_pairs={{0,2},{1,3},{2,4},{3,5},{4,6},{5,7},{6,8},{7,9},{8,10},{9,11},{10,... | collective-permute-start | bytes 1327112 | tf_op jit(solution)/shard_map/ppermute | solution.py:262
  1.2 2.6 %collective-permute-start.2 = (f32[864,128]{1,0:T(8,128)}, f32[864,128]{1,0:T(8,128)S(1)}, u32[]{:S(2)}, u32[]{:S(2)}) collective-permute-start(f32[864,128]{1,0:T(8,128)} %bitcast.12), channel_id=1, source_target_pairs={{0,1},{1,0},{2,3},{3,2},{4,5},{5,4},{6,7},{7,6},{8,9},{9,8},{10,11... | collective-permute-start | bytes 1327112 | tf_op jit(solution)/shard_map/ppermute | solution.py:262
  4.4 1.3 %collective-permute-start = (f32[8,128]{1,0:T(8,128)S(1)}, f32[8,128]{1,0:T(8,128)S(1)}, u32[]{:S(2)}, u32[]{:S(2)}) collective-permute-start(f32[8,128]{1,0:T(8,128)S(1)} %broadcast_in_dim.9.refs_9_), channel_id=1, source_target_pairs={{0,2},{1,3},{2,4},{3,5},{4,6},{5,7},{6,8},{7,9},{8,10},{9,11},{10,... | collective-permute-start | bytes 12296 | tf_op jit(solution)/shard_map/ppermute | solution.py:262
  5.7 0.5 %collective-permute-start.3 = (f32[8,128]{1,0:T(8,128)S(1)}, f32[8,128]{1,0:T(8,128)S(1)}, u32[]{:S(2)}, u32[]{:S(2)}) collective-permute-start(f32[8,128]{1,0:T(8,128)S(1)} %broadcast_in_dim.9.refs_9_), channel_id=1, source_target_pairs={{0,1},{1,0},{2,3},{3,2},{4,5},{5,4},{6,7},{7,6},{8,9},{9,8},{10,11... | collective-permute-start | bytes 12296 | tf_op jit(solution)/shard_map/ppermute | solution.py:262
  6.2 1.6 %place.1 = (f32[864,128]{1,0:T(8,128)S(1)}, f32[256,256]{1,0:T(8,128)S(1)}, f32[48,144]{1,0:T(8,128)S(1)}, f32[48,144]{1,0:T(8,128)S(1)}, f32[48,72]{1,0:T(8,128...) custom-call(f32[864,128]{1,0:T(8,128)} %bitcast.13, ...), custom_call_target="tpu_custom_call" | custom-call | tf_op jit(solution)/shard_map/place/pallas_call | solution.py:96
  7.8 4.5 %collective-permute-done.1.refs_1_ = f32[864,128]{1,0:T(8,128)S(1)} collective-permute-done((f32[864,128]{1,0:T(8,128)}, f32[864,128]{1,0:T(8,128)S(1)}, u32[]{:S(2)}, u32[]{:S(2)}) %collective-permute-start.1) | collective-permute-done | bytes 442400 | tf_op jit(solution)/shard_map/ppermute | solution.py:262
  12.3 1.8 %shard_map.104 = (f32[864,128]{1,0:T(8,128)S(1)}, f32[864,128]{1,0:T(8,128)S(1)}, f32[32,128]{1,0:T(8,128)S(1)}) custom-call(f32[864,128]{1,0:T(8,128)S(1)} %get-tuple-element.18.refs_0_, f32[864,128]{1,0:T(8,128)S(1)} %collective-permute-done.1.refs_1_, f32[256,256]{1,0:T(8,128)S(1)} %get-tuple-element.19.refs_2_, f32[48,144]{1,0:T(8,128)S(1)} %get-tuple-element.20.refs_3_, ...), custom_call_target="tpu_custom_call" | custom-call | tf_op jit(solution)/shard_map/pallas_call | solution.py:240
  14.2 0.0 collective-permute-done.refs_11_.refs_0_
  14.2 0.0 collective-permute-done.3.refs_10_
  14.2 0.0 collective-permute-done.2.refs_0_
  14.2 1.9 %shard_map.105 = (f32[864,128]{1,0:T(8,128)S(1)}, f32[864,128]{1,0:T(8,128)S(1)}, f32[32,128]{1,0:T(8,128)S(1)}) custom-call(f32[864,128]{1,0:T(8,128)S(1)} %collective-permute-done.2.refs_0_, f32[864,128]{1,0:T(8,128)S(1)} %collective-permute-done.1.refs_1_, f32[256,256]{1,0:T(8,128)S(1)} %get-tuple-element.19.refs_2_, ...), custom_call_target="tpu_custom_call" | custom-call | tf_op jit(solution)/shard_map/pallas_call | solution.py:240
  16.1 2.4 %collective-permute-start.4 = (f32[864,128]{1,0:T(8,128)S(1)}, f32[864,128]{1,0:T(8,128)S(1)}, u32[]{:S(2)}, u32[]{:S(2)}) collective-permute-start(f32[864,128]{1,0:T(8,128)S(1)} %get-tuple-element.29), channel_id=1, source_target_pairs={{0,1},{1,0},{2,3},{3,2},{4,5},{5,4},{6,7},{7,6},{8,9},{9,8},{10,11... | collective-permute-start | bytes 1327112 | tf_op jit(solution)/shard_map/ppermute | solution.py:262
  18.5 3.0 %collective-permute-start.5 = (f32[864,128]{1,0:T(8,128)S(1)}, f32[864,128]{1,0:T(8,128)S(1)}, u32[]{:S(2)}, u32[]{:S(2)}) collective-permute-start(f32[864,128]{1,0:T(8,128)S(1)} %get-tuple-element.30), channel_id=1, source_target_pairs={{0,30},{1,31},{2,0},{3,1},{4,2},{5,3},{6,4},{7,5},{8,6},{9,7},{10,... | collective-permute-start | bytes 1327112 | tf_op jit(solution)/shard_map/ppermute | solution.py:262
  21.5 9.1 %all_to_all.11 = f32[32,1,128]{2,1,0:T(1,128)S(1)} all-to-all(f32[32,1,128]{2,1,0:T(1,128)S(1)} %bitcast.10), channel_id=1, replica_groups=mesh['blk'=16,'grp'=2] {'blk','grp'}, dimensions={0} | all-to-all | bytes 32768 | tf_op jit(solution)/shard_map/all_to_all | solution.py:281
  30.6 0.0 collective-permute-done.4.refs_2_
  30.6 0.0 collective-permute-done.5.refs_3_
  30.6 0.9 %combine.1 = (f32[864,128]{1,0:T(8,128)}, f32[1,1]{1,0:T(1,128)}) custom-call(f32[8,128]{1,0:T(8,128)S(1)} %collective-permute-done.refs_11_.refs_0_, f32[864,128]{1,0:T(8,128)S(1)} %get-tuple-element.26.refs_1_, f32[864,128]{1,0:T(8,128)S(1)} %collective-permute-done.4.refs_2_, f32[864,128]{1,0:T(8,128)S(1)} %collective-permute-done.5.refs_3_, ...), custom_call_target="tpu_custom_call" | custom-call | tf_op jit(solution)/shard_map/combine/pallas_call | solution.py:283
  (1 shorter events, 0.0 us)
Async XLA Ops:
  0.6 11.7 %collective-permute-start.1 = (f32[864,128]{1,0:T(8,128)}, f32[864,128]{1,0:T(8,128)S(1)}, u32[]{:S(2)}, u32[]{:S(2)}) collective-permute-start(f32[864,128]{1,0:T(8,128)} %bitcast.11), channel_id=1, source_target_pairs={{0,2},{1,3},{2,4},{3,5},{4,6},{5,7},{6,8},{7,9},{8,10},{9,11},{10,... | collective-permute-start | bytes 1327112 | tf_op jit(solution)/shard_map/ppermute | solution.py:262
  1.2 13.0 %collective-permute-start.2 = (f32[864,128]{1,0:T(8,128)}, f32[864,128]{1,0:T(8,128)S(1)}, u32[]{:S(2)}, u32[]{:S(2)}) collective-permute-start(f32[864,128]{1,0:T(8,128)} %bitcast.12), channel_id=1, source_target_pairs={{0,1},{1,0},{2,3},{3,2},{4,5},{5,4},{6,7},{7,6},{8,9},{9,8},{10,11... | collective-permute-start | bytes 1327112 | tf_op jit(solution)/shard_map/ppermute | solution.py:262
  4.4 9.8 %collective-permute-start = (f32[8,128]{1,0:T(8,128)S(1)}, f32[8,128]{1,0:T(8,128)S(1)}, u32[]{:S(2)}, u32[]{:S(2)}) collective-permute-start(f32[8,128]{1,0:T(8,128)S(1)} %broadcast_in_dim.9.refs_9_), channel_id=1, source_target_pairs={{0,2},{1,3},{2,4},{3,5},{4,6},{5,7},{6,8},{7,9},{8,10},{9,11},{10,... | collective-permute-start | bytes 12296 | tf_op jit(solution)/shard_map/ppermute | solution.py:262
  5.7 8.5 %collective-permute-start.3 = (f32[8,128]{1,0:T(8,128)S(1)}, f32[8,128]{1,0:T(8,128)S(1)}, u32[]{:S(2)}, u32[]{:S(2)}) collective-permute-start(f32[8,128]{1,0:T(8,128)S(1)} %broadcast_in_dim.9.refs_9_), channel_id=1, source_target_pairs={{0,1},{1,0},{2,3},{3,2},{4,5},{5,4},{6,7},{7,6},{8,9},{9,8},{10,11... | collective-permute-start | bytes 12296 | tf_op jit(solution)/shard_map/ppermute | solution.py:262
  16.1 14.6 %collective-permute-start.4 = (f32[864,128]{1,0:T(8,128)S(1)}, f32[864,128]{1,0:T(8,128)S(1)}, u32[]{:S(2)}, u32[]{:S(2)}) collective-permute-start(f32[864,128]{1,0:T(8,128)S(1)} %get-tuple-element.29), channel_id=1, source_target_pairs={{0,1},{1,0},{2,3},{3,2},{4,5},{5,4},{6,7},{7,6},{8,9},{9,8},{10,11... | collective-permute-start | bytes 1327112 | tf_op jit(solution)/shard_map/ppermute | solution.py:262
  18.5 12.2 %collective-permute-start.5 = (f32[864,128]{1,0:T(8,128)S(1)}, f32[864,128]{1,0:T(8,128)S(1)}, u32[]{:S(2)}, u32[]{:S(2)}) collective-permute-start(f32[864,128]{1,0:T(8,128)S(1)} %get-tuple-element.30), channel_id=1, source_target_pairs={{0,30},{1,31},{2,0},{3,1},{4,2},{5,3},{6,4},{7,5},{8,6},{9,7},{10,... | collective-permute-start | bytes 1327112 | tf_op jit(solution)/shard_map/ppermute | solution.py:262

commit v5 on v4

--- a/solution.py
+++ b/solution.py
@@ -13,6 +13,7 @@
 LANES = 128
 F32 = jnp.float32
 PAD = 8
+PARTS = 4
 LIMIT = 12 * 1024 * 1024
 
 
@@ -247,9 +248,19 @@
     )(*operands)
 
 
-def combine_body(scale, e_scale, w_ref, mine_ref, back_ref, behind_ref, everyone_ref, out_ref, e_ref):
-    out_ref[...] = scale * (w_ref[:1, :] * mine_ref[...] + back_ref[...] + behind_ref[...])
-    e_ref[...] = e_scale * jnp.sum(everyone_ref[...], axis=0, keepdims=True)[:, :1]
+def combine_body(scale, e_scale, w_ref, mine_ref, back_ref, behind_ref, everyone_ref, out_ref, e_ref, sum_ref, e_sum_ref, sems):
+    count = sems.shape[0] - 1
+    size = sum_ref.shape[0] // count
+    e_sum_ref[...] = e_scale * jnp.sum(everyone_ref[...], axis=0, keepdims=True)[:, :1]
+    copies = [pltpu.make_async_copy(e_sum_ref, e_ref, sems.at[count])]
+    copies[0].start()
+    for i in range(count):
+        at = pl.ds(i * size, size)
+        sum_ref[at, :] = scale * (w_ref[:1, :] * mine_ref[at, :] + back_ref[at, :] + behind_ref[at, :])
+        copies.append(pltpu.make_async_copy(sum_ref.at[at], out_ref.at[at], sems.at[i]))
+        copies[-1].start()
+    for copy in copies:
+        copy.wait()
 
 
 AXES = ("blk", "grp")
@@ -283,7 +294,9 @@
     exchange, energy = pl.pallas_call(
         lambda *refs: combine_body(-mixing, -2.0 * mixing / (2.0 * cells * count), *refs),
         out_shape=(jax.ShapeDtypeStruct(own.shape, F32), jax.ShapeDtypeStruct((1, 1), F32)),
-        in_specs=[vm] * 5, out_specs=(vm, vm),
+        in_specs=[vm] * 5, out_specs=[pl.BlockSpec(memory_space=pltpu.HBM)] * 2,
+        scratch_shapes=[pltpu.VMEM(own.shape, F32), pltpu.VMEM((1, 1), F32),
+                        pltpu.SemaphoreType.DMA((math.gcd(own.shape[0] // 8, PARTS) + 1,))],
         compiler_params=pltpu.CompilerParams(vmem_limit_bytes=LIMIT),
         name="combine",
     )(w_previous, mine, back, behind, everyone)

time: 31.7 us -> 31.7 us (level)
  no operation moved by 1% of the time
where the time goes in v5:
time: 31.7 us; the launch traced here: 31.5 us
  starting transfers between devices  10.4 us (33%)
  blocking collectives  9.12 us (29%)
  Pallas kernels  6.14 us (19%)
  waiting for transfers between devices  4.54 us (14%)
  between operations  1.34 us (4%)
    ppermute x6, starting transfers between devices, moved(): return lax.ppermute(value, AXES, pairs)  10.4 us
    all_to_all x1, blocking collectives, local(): everyone = lax.all_to_all(share, AXES, 0, 0, tiled=True)  9.12 us
    ppermute x6, waiting for transfers between devices, moved(): return lax.ppermute(value, AXES, pairs)  4.54 us
    pallas_call x2, Pallas kernels, pair_call(): pl.pallas_call(lambda *refs: pair_body(extent, 1 if more else 0, *refs),...  3.72 us
    pallas_call x1, Pallas kernels, placed(): pl.pallas_call(lambda *refs: place_body(len(arrays), variants, *refs), ou...  1.57 us
    pallas_call x1, Pallas kernels, local(): pl.pallas_call(lambda *refs: combine_body(-mixing, -2.0 * mixing / (2.0 *...  0.85 us
  transfers between devices with their start and end apart: 6, of which 1 were waited for; matrix products, arithmetic and copies ran while one was open for 0% of the time, Pallas kernels for 11%

profile of v5, /device:TPU:0, one launch (start us, length us, event | category | flops | bytes accessed | tf_op | source)
XLA Modules:
  0.0 31.5 jit_solution(7018845255789039404)
XLA Ops:
  0.6 0.5 %collective-permute-start.1 = (f32[864,128]{1,0:T(8,128)}, f32[864,128]{1,0:T(8,128)S(1)}, u32[]{:S(2)}, u32[]{:S(2)}) collective-permute-start(f32[864,128]{1,0:T(8,128)} %bitcast.11), channel_id=1, source_target_pairs={{0,2},{1,3},{2,4},{3,5},{4,6},{5,7},{6,8},{7,9},{8,10},{9,11},{10,... | collective-permute-start | bytes 1327112 | tf_op jit(solution)/shard_map/ppermute | solution.py:273
  1.2 2.6 %collective-permute-start.2 = (f32[864,128]{1,0:T(8,128)}, f32[864,128]{1,0:T(8,128)S(1)}, u32[]{:S(2)}, u32[]{:S(2)}) collective-permute-start(f32[864,128]{1,0:T(8,128)} %bitcast.12), channel_id=1, source_target_pairs={{0,1},{1,0},{2,3},{3,2},{4,5},{5,4},{6,7},{7,6},{8,9},{9,8},{10,11... | collective-permute-start | bytes 1327112 | tf_op jit(solution)/shard_map/ppermute | solution.py:273
  4.4 1.3 %collective-permute-start = (f32[8,128]{1,0:T(8,128)S(1)}, f32[8,128]{1,0:T(8,128)S(1)}, u32[]{:S(2)}, u32[]{:S(2)}) collective-permute-start(f32[8,128]{1,0:T(8,128)S(1)} %broadcast_in_dim.9.refs_9_), channel_id=1, source_target_pairs={{0,2},{1,3},{2,4},{3,5},{4,6},{5,7},{6,8},{7,9},{8,10},{9,11},{10,... | collective-permute-start | bytes 12296 | tf_op jit(solution)/shard_map/ppermute | solution.py:273
  5.7 0.5 %collective-permute-start.3 = (f32[8,128]{1,0:T(8,128)S(1)}, f32[8,128]{1,0:T(8,128)S(1)}, u32[]{:S(2)}, u32[]{:S(2)}) collective-permute-start(f32[8,128]{1,0:T(8,128)S(1)} %broadcast_in_dim.9.refs_9_), channel_id=1, source_target_pairs={{0,1},{1,0},{2,3},{3,2},{4,5},{5,4},{6,7},{7,6},{8,9},{9,8},{10,11... | collective-permute-start | bytes 12296 | tf_op jit(solution)/shard_map/ppermute | solution.py:273
  6.2 1.6 %place.1 = (f32[864,128]{1,0:T(8,128)S(1)}, f32[256,256]{1,0:T(8,128)S(1)}, f32[48,144]{1,0:T(8,128)S(1)}, f32[48,144]{1,0:T(8,128)S(1)}, f32[48,72]{1,0:T(8,128...) custom-call(f32[864,128]{1,0:T(8,128)} %bitcast.13, ...), custom_call_target="tpu_custom_call" | custom-call | tf_op jit(solution)/shard_map/place/pallas_call | solution.py:97
  7.8 4.5 %collective-permute-done.1.refs_1_ = f32[864,128]{1,0:T(8,128)S(1)} collective-permute-done((f32[864,128]{1,0:T(8,128)}, f32[864,128]{1,0:T(8,128)S(1)}, u32[]{:S(2)}, u32[]{:S(2)}) %collective-permute-start.1) | collective-permute-done | bytes 442400 | tf_op jit(solution)/shard_map/ppermute | solution.py:273
  12.3 1.8 %shard_map.104 = (f32[864,128]{1,0:T(8,128)S(1)}, f32[864,128]{1,0:T(8,128)S(1)}, f32[32,128]{1,0:T(8,128)S(1)}) custom-call(f32[864,128]{1,0:T(8,128)S(1)} %get-tuple-element.18.refs_0_, f32[864,128]{1,0:T(8,128)S(1)} %collective-permute-done.1.refs_1_, f32[256,256]{1,0:T(8,128)S(1)} %get-tuple-element.19.refs_2_, f32[48,144]{1,0:T(8,128)S(1)} %get-tuple-element.20.refs_3_, ...), custom_call_target="tpu_custom_call" | custom-call | tf_op jit(solution)/shard_map/pallas_call | solution.py:241
  14.2 0.0 collective-permute-done.refs_11_.refs_0_
  14.2 0.0 collective-permute-done.3.refs_10_
  14.2 0.0 collective-permute-done.2.refs_0_
  14.2 1.9 %shard_map.105 = (f32[864,128]{1,0:T(8,128)S(1)}, f32[864,128]{1,0:T(8,128)S(1)}, f32[32,128]{1,0:T(8,128)S(1)}) custom-call(f32[864,128]{1,0:T(8,128)S(1)} %collective-permute-done.2.refs_0_, f32[864,128]{1,0:T(8,128)S(1)} %collective-permute-done.1.refs_1_, f32[256,256]{1,0:T(8,128)S(1)} %get-tuple-element.19.refs_2_, ...), custom_call_target="tpu_custom_call" | custom-call | tf_op jit(solution)/shard_map/pallas_call | solution.py:241
  16.1 2.4 %collective-permute-start.4 = (f32[864,128]{1,0:T(8,128)S(1)}, f32[864,128]{1,0:T(8,128)S(1)}, u32[]{:S(2)}, u32[]{:S(2)}) collective-permute-start(f32[864,128]{1,0:T(8,128)S(1)} %get-tuple-element.29), channel_id=1, source_target_pairs={{0,1},{1,0},{2,3},{3,2},{4,5},{5,4},{6,7},{7,6},{8,9},{9,8},{10,11... | collective-permute-start | bytes 1327112 | tf_op jit(solution)/shard_map/ppermute | solution.py:273
  18.5 3.0 %collective-permute-start.5 = (f32[864,128]{1,0:T(8,128)S(1)}, f32[864,128]{1,0:T(8,128)S(1)}, u32[]{:S(2)}, u32[]{:S(2)}) collective-permute-start(f32[864,128]{1,0:T(8,128)S(1)} %get-tuple-element.30), channel_id=1, source_target_pairs={{0,30},{1,31},{2,0},{3,1},{4,2},{5,3},{6,4},{7,5},{8,6},{9,7},{10,... | collective-permute-start | bytes 1327112 | tf_op jit(solution)/shard_map/ppermute | solution.py:273
  21.5 9.1 %all_to_all.11 = f32[32,1,128]{2,1,0:T(1,128)S(1)} all-to-all(f32[32,1,128]{2,1,0:T(1,128)S(1)} %bitcast.10), channel_id=1, replica_groups=mesh['blk'=16,'grp'=2] {'blk','grp'}, dimensions={0} | all-to-all | bytes 32768 | tf_op jit(solution)/shard_map/all_to_all | solution.py:292
  30.6 0.0 collective-permute-done.4.refs_2_
  30.6 0.0 collective-permute-done.5.refs_3_
  30.6 0.8 %combine.1 = (f32[864,128]{1,0:T(8,128)}, f32[1,1]{1,0:T(1,128)}) custom-call(f32[8,128]{1,0:T(8,128)S(1)} %collective-permute-done.refs_11_.refs_0_, f32[864,128]{1,0:T(8,128)S(1)} %get-tuple-element.26.refs_1_, f32[864,128]{1,0:T(8,128)S(1)} %collective-permute-done.4.refs_2_, f32[864,128]{1,0:T(8,128)S(1)} %collective-permute-done.5.refs_3_, ...), custom_call_target="tpu_custom_call" | custom-call | tf_op jit(solution)/shard_map/combine/pallas_call | solution.py:294
  (1 shorter events, 0.0 us)
Async XLA Ops:
  0.6 11.7 %collective-permute-start.1 = (f32[864,128]{1,0:T(8,128)}, f32[864,128]{1,0:T(8,128)S(1)}, u32[]{:S(2)}, u32[]{:S(2)}) collective-permute-start(f32[864,128]{1,0:T(8,128)} %bitcast.11), channel_id=1, source_target_pairs={{0,2},{1,3},{2,4},{3,5},{4,6},{5,7},{6,8},{7,9},{8,10},{9,11},{10,... | collective-permute-start | bytes 1327112 | tf_op jit(solution)/shard_map/ppermute | solution.py:273
  1.2 13.0 %collective-permute-start.2 = (f32[864,128]{1,0:T(8,128)}, f32[864,128]{1,0:T(8,128)S(1)}, u32[]{:S(2)}, u32[]{:S(2)}) collective-permute-start(f32[864,128]{1,0:T(8,128)} %bitcast.12), channel_id=1, source_target_pairs={{0,1},{1,0},{2,3},{3,2},{4,5},{5,4},{6,7},{7,6},{8,9},{9,8},{10,11... | collective-permute-start | bytes 1327112 | tf_op jit(solution)/shard_map/ppermute | solution.py:273
  4.4 9.8 %collective-permute-start = (f32[8,128]{1,0:T(8,128)S(1)}, f32[8,128]{1,0:T(8,128)S(1)}, u32[]{:S(2)}, u32[]{:S(2)}) collective-permute-start(f32[8,128]{1,0:T(8,128)S(1)} %broadcast_in_dim.9.refs_9_), channel_id=1, source_target_pairs={{0,2},{1,3},{2,4},{3,5},{4,6},{5,7},{6,8},{7,9},{8,10},{9,11},{10,... | collective-permute-start | bytes 12296 | tf_op jit(solution)/shard_map/ppermute | solution.py:273
  5.7 8.5 %collective-permute-start.3 = (f32[8,128]{1,0:T(8,128)S(1)}, f32[8,128]{1,0:T(8,128)S(1)}, u32[]{:S(2)}, u32[]{:S(2)}) collective-permute-start(f32[8,128]{1,0:T(8,128)S(1)} %broadcast_in_dim.9.refs_9_), channel_id=1, source_target_pairs={{0,1},{1,0},{2,3},{3,2},{4,5},{5,4},{6,7},{7,6},{8,9},{9,8},{10,11... | collective-permute-start | bytes 12296 | tf_op jit(solution)/shard_map/ppermute | solution.py:273
  16.1 14.6 %collective-permute-start.4 = (f32[864,128]{1,0:T(8,128)S(1)}, f32[864,128]{1,0:T(8,128)S(1)}, u32[]{:S(2)}, u32[]{:S(2)}) collective-permute-start(f32[864,128]{1,0:T(8,128)S(1)} %get-tuple-element.29), channel_id=1, source_target_pairs={{0,1},{1,0},{2,3},{3,2},{4,5},{5,4},{6,7},{7,6},{8,9},{9,8},{10,11... | collective-permute-start | bytes 1327112 | tf_op jit(solution)/shard_map/ppermute | solution.py:273
  18.5 12.2 %collective-permute-start.5 = (f32[864,128]{1,0:T(8,128)S(1)}, f32[864,128]{1,0:T(8,128)S(1)}, u32[]{:S(2)}, u32[]{:S(2)}) collective-permute-start(f32[864,128]{1,0:T(8,128)S(1)} %get-tuple-element.30), channel_id=1, source_target_pairs={{0,30},{1,31},{2,0},{3,1},{4,2},{5,3},{6,4},{7,5},{8,6},{9,7},{10,... | collective-permute-start | bytes 1327112 | tf_op jit(solution)/shard_map/ppermute | solution.py:273
